TPU v7x, 32 devices: a whole 2x2x4 slice. The times are simulated.
32 devices in a mesh: parts: 2 (over y), branch: 2 (over x), seq: 4 (over z), head: 2 (over core).
Axes of the slice: x: 2, y: 2, z: 4, core: 2. Of those that a mesh axis runs over, the one named last changes fastest.
Arguments:
- queries: bfloat16 [4, 48, 8, 128], P(('parts', 'branch'), 'seq', 'head'), parts along dimension 0, may hold values from -160 to 160
- output_cotangent: bfloat16 [4, 48, 8, 128], P(('parts', 'branch'), 'seq', 'head'), parts along dimension 0, may hold values from -6 to 6
- root_keys: bfloat16 [4096, 128], P(('parts', 'seq')), parts along dimension 0, may hold values from -8 to 8
- root_values: bfloat16 [4096, 128], P(('parts', 'seq')), parts along dimension 0, may hold values from -6 to 6
- branch_keys: bfloat16 [4, 2048, 128], P(('parts', 'branch'), 'seq'), parts along dimension 0, may hold values from -6 to 6
- branch_values: bfloat16 [4, 2048, 128], P(('parts', 'branch'), 'seq'), parts along dimension 0, may hold values from -6 to 6
- answer_positions: int32 [4, 48], P(('parts', 'branch')), parts along dimension 0, may hold values from 0 to 2047, as said below
Outputs:
- attention: bfloat16 [4, 48, 8, 128], P(('parts', 'branch'), 'seq', 'head'), parts along dimension 0
- query_gradient: float32 [4, 48, 8, 128], P(('parts', 'branch'), 'seq', 'head'), parts along dimension 0
- root_key_gradient: float32 [4096, 128], P(('parts', 'seq')), parts along dimension 0
- root_value_gradient: float32 [4096, 128], P(('parts', 'seq')), parts along dimension 0
- branch_key_gradient: float32 [4, 2048, 128], P(('parts', 'branch'), 'seq'), parts along dimension 0
- branch_value_gradient: float32 [4, 2048, 128], P(('parts', 'branch'), 'seq'), parts along dimension 0
There are 2 independent parts, one for each index of `parts`. A program takes and returns all parts, laid end to end along the dimension named above; each array names one. Nothing has to cross between parts.
Inputs may be any that keep to these rules, and one draw needn't show every extreme that they name: `answer_positions`: within each branch the positions are strictly increasing.
All inputs are finite; a program needn't handle non-finite values.
Results may differ from a plain program's by a relative error of at most 0.015.
Values may be sent and summed in bfloat16 or wider, within the bound.
No kernel may reach another device: no remote copies, remote signals or barrier semaphores. Data moves between devices by JAX's collectives and lax.ppermute only.
A program may use at most 64 MiB of HBM per device.

v0:
```python
import functools
import math

import jax
import jax.numpy as jnp
from jax import lax
from jax.experimental import pallas as pl
from jax.experimental.pallas import tpu as pltpu
from jax.sharding import PartitionSpec as P

NEG = -1e30
LOG2E = math.log2(math.e)
LANES = 128

bf16 = jnp.bfloat16
f32 = jnp.float32


def nt(left, right):
    return lax.dot_general(left, right, (((1,), (1,)), ((), ())), preferred_element_type=f32)


def nn(left, right):
    return jnp.dot(left, right, preferred_element_type=f32)


def total_of(values):
    return functools.reduce(jnp.add, values)


def cut(total, most):
    if total <= most:
        return [(0, total)]
    size = most
    while total % size or size % LANES:
        size -= LANES
        if size <= 0:
            return [(0, total)]
    return [(at, size) for at in range(0, total, size)]


def lane_tiles(rows):
    tiles = -(-rows // LANES)
    return tiles + tiles % 2


def arrange(place, source, base, query, grad, offset, lay):
    for target in range(lay.count):
        spot = place ^ target
        at = jnp.int32(0)
        for step, bit in enumerate(lay.bits):
            at = at + (((spot >> bit) & 1) << step)
        start = pl.multiple_of(base + at * (2 * lay.rows), 16)
        to = pl.multiple_of(offset + target * lay.rows, 16)
        query[pl.ds(to, lay.rows), :] = source[pl.ds(start, lay.rows), :]
        start = pl.multiple_of(base + at * (2 * lay.rows) + lay.rows, 16)
        grad[pl.ds(to, lay.rows), :] = source[pl.ds(start, lay.rows), :]


def split3(value):
    high = value.astype(bf16).astype(f32)
    rest = value - high
    middle = rest.astype(bf16).astype(f32)
    low = (rest - middle).astype(bf16).astype(f32)
    return high, middle, low


def forward_kernel(gathered, root_k, root_v, branch_k, branch_v, places,
                   own, coded, *rest, lay):
    messages, (vectors, query_rows, grad_rows) = rest[:-3], rest[-3:]
    place = lax.axis_index("seq")
    rows, total, tiles = lay.rows, lay.total, lay.tiles
    arrange(place, gathered, 0, query_rows, grad_rows, 0, lay)
    branch_count = branch_k.shape[0]
    rk, rv, bk, bv = root_k[...], root_v[...], branch_k[...], branch_v[...]
    stat_columns = []
    for at, size in cut(total, 384):
        query = query_rows[at:at + size, :]
        grad = grad_rows[at:at + size, :]
        root_s = nt(query, rk) * (lay.scale * LOG2E)
        branch_s = nt(query, bk) * (lay.scale * LOG2E)
        key_place = place * branch_count + lax.broadcasted_iota(jnp.int32, (size, branch_count), 1)
        branch_s = jnp.where(key_place <= places[at:at + size, :], branch_s, NEG)
        peak = jnp.maximum(jnp.max(root_s, axis=1, keepdims=True),
                           jnp.max(branch_s, axis=1, keepdims=True))
        root_p = jnp.exp2(root_s - peak)
        branch_p = jnp.exp2(branch_s - peak)
        norm = jnp.sum(root_p, axis=1, keepdims=True) + jnp.sum(branch_p, axis=1, keepdims=True)
        root_d = nt(grad, rv)
        branch_d = nt(grad, bv)
        inverse = 1.0 / norm
        delta = (jnp.sum(root_p * root_d, axis=1, keepdims=True)
                 + jnp.sum(branch_p * branch_d, axis=1, keepdims=True)) * inverse
        root_t = (root_p * (root_d - delta)).astype(bf16)
        branch_t = (branch_p * (branch_d - delta)).astype(bf16)
        root_p = root_p.astype(bf16)
        branch_p = branch_p.astype(bf16)
        vectors[0, at:at + size, :] = (nn(root_p, rv) + nn(branch_p, bv)) * inverse
        vectors[1, at:at + size, :] = (nn(root_t, rk) + nn(branch_t, bk)) * inverse
        vectors[2, at:at + size, :] = (nn(root_p, rk) + nn(branch_p, bk)) * inverse
        lse = peak + jnp.log(norm) * LOG2E
        lane = lax.broadcasted_iota(jnp.int32, (size, LANES), 1)
        packed = jnp.zeros((size, LANES), f32)
        for spot, piece in enumerate(split3(lse) + split3(delta)):
            packed = jnp.where(lane == spot, piece, packed)
        stat_columns.append(packed)
    if tiles * LANES > total:
        stat_columns.append(jnp.zeros((tiles * LANES - total, LANES), f32))
    columns = jnp.concatenate(stat_columns, axis=0)
    stats = [columns[k * LANES:(k + 1) * LANES, :].T[0:8, :] for k in range(tiles)]
    for k in range(tiles):
        coded[:, k * LANES:(k + 1) * LANES] = stats[k]
    stat_rows = jnp.concatenate(stats, axis=0).astype(bf16)

    def piece(which, target):
        return vectors[which, pl.ds(pl.multiple_of(target * rows, 16), rows), :]

    for which in range(3):
        span = slice(which * rows, (which + 1) * rows)
        own[span, :] = piece(which, place)
        if lay.swap:
            for m, message in enumerate(messages):
                message[span, :] = piece(which, place ^ (m + 1)).astype(bf16)
        else:
            for target in range(lay.count):
                messages[0][target, span, :] = piece(which, target).astype(bf16)
    if lay.swap:
        for message in messages:
            message[3 * rows:, :] = stat_rows
    else:
        for target in range(lay.count):
            messages[0][target, 3 * rows:, :] = stat_rows


def combine_kernel(coded, *rest, lay):
    messages, final, every = rest[:-2], rest[-2], rest[-1]
    rows, count = lay.rows, lay.count
    final[...] = jnp.zeros(final.shape, f32)
    every[...] = jnp.zeros(every.shape, f32)
    for k in range(lay.tiles):
        span = slice(k * LANES, (k + 1) * LANES)
        stats = [coded[:, span]]
        for message in messages:
            both = message[3 * rows + 16 * (k // 2):3 * rows + 16 * (k // 2) + 16, :].astype(f32)
            stats.append(both[8 * (k % 2):8 * (k % 2) + 8, :])
        lses = [s[0:1] + s[1:2] + s[2:3] for s in stats]
        deltas = [s[3:4] + s[4:5] + s[5:6] for s in stats]
        peak = functools.reduce(jnp.maximum, lses)
        shares = [jnp.exp2(v - peak) for v in lses]
        norm = total_of(shares)
        final[0:1, span] = peak + jnp.log(norm) * LOG2E
        final[1:2, span] = total_of([a * b for a, b in zip(shares, deltas)]) / norm
        for v in range(count):
            every[v:v + 1, span] = lses[v]
            every[count + v:count + v + 1, span] = deltas[v]


def local_weights(parts, query, grad, probs, slopes, local, line, logits, products, scale):
    block = 256
    for row, width in cut(query.shape[0], 384):
        lanes = slice(row, row + width)
        q, g = query[lanes, :], grad[lanes, :]
        peak = jnp.full((1, width), NEG, f32)
        spots = []
        for start, keys, values, visible in parts:
            for at in range(0, keys.shape[0], block):
                size = min(block, keys.shape[0] - at)
                s = nt(keys[at:at + size, :], q) * (scale * LOG2E)
                if visible is not None:
                    s = jnp.where(visible(at, size, lanes), s, NEG)
                logits[start + at:start + at + size, 0:width] = s
                products[start + at:start + at + size, 0:width] = nt(values[at:at + size, :], g)
                peak = jnp.maximum(peak, jnp.max(s, axis=0, keepdims=True))
                spots.append(slice(start + at, start + at + size))
        norm = jnp.zeros((1, width), f32)
        weighted = jnp.zeros((1, width), f32)
        for spot in spots:
            p = jnp.exp2(logits[spot, 0:width] - peak)
            logits[spot, 0:width] = p
            probs[spot, lanes] = p.astype(bf16)
            norm = norm + jnp.sum(p, axis=0, keepdims=True)
            weighted = weighted + jnp.sum(p * products[spot, 0:width], axis=0, keepdims=True)
        delta = weighted / norm
        for spot in spots:
            slopes[spot, lanes] = (logits[spot, 0:width] * (products[spot, 0:width] - delta)).astype(bf16)
        local[line:line + 1, lanes] = peak
        local[line + 1:line + 2, lanes] = delta


def own_pre_kernel(mine, other, places, root_k, root_v, branch_k, branch_v,
                   probs, slopes, local, query, grad, logits, products, *, lay):
    place, half = lax.axis_index("seq"), lax.axis_index("head")
    arrange(place, mine, 0, query, grad, half * lay.total, lay)
    arrange(place, other, 0, query, grad, (1 - half) * lay.total, lay)
    count = branch_k.shape[0]

    def visible(at, size, lanes):
        spot = (place * count + at) + lax.broadcasted_iota(jnp.int32, (size, lanes.stop - lanes.start), 0)
        return spot <= places[0:1, lanes]

    local_weights([(0, branch_k, branch_v, visible)], query, grad, probs, slopes, local, 0,
                  logits, products, lay.scale)
    local_weights([(count, root_k, root_v, None)], query, grad, probs, slopes, local, 2,
                  logits, products, lay.scale)


def other_pre_kernel(pair, root_k, root_v, probs, slopes, local, query, grad,
                     logits, products, *, lay):
    place, half = lax.axis_index("seq"), lax.axis_index("head")
    arrange(place, pair, 0, query, grad, half * lay.total, lay)
    arrange(place, pair, 2 * lay.total, query, grad, (1 - half) * lay.total, lay)
    local_weights([(0, root_k, root_v, None)], query, grad, probs, slopes, local, 2,
                  logits, products, lay.scale)


def scaled_rows(local, line, stats, query, grad, both, single, scale):
    for k in range(query.shape[0] // LANES):
        span = slice(k * LANES, (k + 1) * LANES)
        weight = jnp.exp2(local[line:line + 1, span] - stats[0:1, span])
        shift = weight * (local[line + 1:line + 2, span] - stats[1:2, span])
        stacked = jnp.concatenate([weight, shift, jnp.zeros((LANES - 2, LANES), f32)], axis=0)
        columns = stacked.T
        weight, shift = columns[:, 0:1], columns[:, 1:2]
        q = query[span, :].astype(f32) * scale
        both[span, 0:LANES] = (grad[span, :].astype(f32) * weight).astype(bf16)
        both[span, LANES:] = (q * shift).astype(bf16)
        single[span, :] = (q * weight).astype(bf16)


def gradients(probs, slopes, spot, both, single):
    wide = nn(probs[spot, :], both[...])
    return wide[:, LANES:] + nn(slopes[spot, :], single[...]), wide[:, 0:LANES]


def own_final_kernel(probs, slopes, local, query, grad, stats, own, every, *rest, lay):
    messages = rest[:lay.count - 1]
    (acc_k, acc_v, out_a, out_q, out_k, out_v, both, single, columns,
     hold_a, hold_q, hold_k, hold_v, sems) = rest[lay.count - 1:]
    rows, count = lay.rows, lay.count
    copies = []

    def send(source, target, sem):
        copies.append(pltpu.make_async_copy(source, target, sem))
        copies[-1].start()

    tall = every.shape[0]
    for k in range(lay.tiles):
        piece = every[:, k * LANES:(k + 1) * LANES]
        if tall < LANES:
            piece = jnp.concatenate([piece, jnp.zeros((LANES - tall, LANES), f32)], axis=0)
        columns[k * LANES:(k + 1) * LANES, :] = piece.T
    mine_rows = columns[pl.ds(pl.multiple_of(lax.axis_index("seq") * rows, 16), rows), :]
    lses = [mine_rows[:, v:v + 1] for v in range(count)]
    deltas = [mine_rows[:, count + v:count + v + 1] for v in range(count)]
    peak = functools.reduce(jnp.maximum, lses)
    shares = [jnp.exp2(v - peak) for v in lses]
    inverse = 1.0 / total_of(shares)
    shares = [s * inverse for s in shares]
    delta = total_of([a * b for a, b in zip(shares, deltas)])
    attended = jnp.zeros((rows, LANES), f32)
    slope_sum = jnp.zeros((rows, LANES), f32)
    for v in range(count):
        source = own if v == 0 else messages[v - 1]
        o_part = source[0:rows, :].astype(f32)
        a_part = source[rows:2 * rows, :].astype(f32)
        b_part = source[2 * rows:3 * rows, :].astype(f32)
        attended = attended + shares[v] * o_part
        slope_sum = slope_sum + shares[v] * (a_part + (deltas[v] - delta) * b_part)
    hold_a[...] = attended.reshape(out_a.shape).astype(bf16)
    send(hold_a, out_a, sems.at[2, 0])
    hold_q[...] = (slope_sum * lay.scale).reshape(out_q.shape)
    send(hold_q, out_q, sems.at[2, 1])

    branch_count = hold_k.shape[0]
    block = 256
    scaled_rows(local, 0, stats, query, grad, both, single, lay.scale)
    for n, at in enumerate(range(0, branch_count, block)):
        spot = slice(at, min(at + block, branch_count))
        hold_k[spot, :], hold_v[spot, :] = gradients(probs, slopes, spot, both, single)
        send(hold_k.at[spot, :], out_k.at[spot, :], sems.at[0, n])
        send(hold_v.at[spot, :], out_v.at[spot, :], sems.at[1, n])
    scaled_rows(local, 2, stats, query, grad, both, single, lay.scale)
    for at in range(0, acc_k.shape[0], block):
        size = min(block, acc_k.shape[0] - at)
        acc_k[at:at + size, :], acc_v[at:at + size, :] = gradients(
            probs, slopes, slice(branch_count + at, branch_count + at + size), both, single)
    for copy in copies:
        copy.wait()


def other_final_kernel(probs, slopes, local, query, grad, stats, acc_k, acc_v, out_k, out_v,
                       both, single, hold_k, hold_v, sems, *, lay):
    scaled_rows(local, 2, stats, query, grad, both, single, lay.scale)
    count = hold_k.shape[0]
    copies = []
    block = 256
    for n, at in enumerate(range(0, count, block)):
        spot = slice(at, min(at + block, count))
        more_k, more_v = gradients(probs, slopes, spot, both, single)
        hold_k[spot, :] = acc_k[spot, :] + more_k
        copies.append(pltpu.make_async_copy(hold_k.at[spot, :], out_k.at[spot, :], sems.at[0, n]))
        copies[-1].start()
        hold_v[spot, :] = acc_v[spot, :] + more_v
        copies.append(pltpu.make_async_copy(hold_v.at[spot, :], out_v.at[spot, :], sems.at[1, n]))
        copies[-1].start()
    for copy in copies:
        copy.wait()


class Lay:
    def __init__(self, count, rows, scale):
        self.count, self.rows, self.scale = count, rows, scale
        self.total = count * rows
        self.tiles = lane_tiles(self.total)
        self.bits = list(reversed(range(count.bit_length() - 1)))
        self.swap = count <= 4


VMEM = pl.BlockSpec(memory_space=pltpu.VMEM)
ANY = pl.BlockSpec(memory_space=pl.ANY)


def call(kernel, lay, args, outs, scratch=(), away=0):
    specs = [VMEM] * (len(outs) - away) + [ANY] * away
    limit = (20 if lay.total <= 384 else 50) * 2**20
    return pl.pallas_call(
        functools.partial(kernel, lay=lay),
        out_shape=[jax.ShapeDtypeStruct(shape, kind) for shape, kind in outs],
        in_specs=[VMEM] * len(args), out_specs=specs, scratch_shapes=list(scratch),
        compiler_params=pltpu.CompilerParams(vmem_limit_bytes=limit),
    )(*args)


def per_device(mesh, queries, output_cotangent, root_keys, root_values,
               branch_keys, branch_values, answer_positions):
    return body(mesh, queries, output_cotangent, root_keys, root_values,
                branch_keys, branch_values, answer_positions)


def body(mesh, queries, output_cotangent, root_keys, root_values,
         branch_keys, branch_values, answer_positions):
    count, branches, heads = mesh.shape["seq"], mesh.shape["branch"], mesh.shape["head"]
    _, answers_here, heads_here, width = queries.shape
    rows = answers_here * heads_here
    lay = Lay(count, rows, 1.0 / math.sqrt(width))
    total, tiles = lay.total, lay.tiles
    lanes = heads * total
    root_count = root_keys.shape[0]
    branch_count = branch_keys.shape[1]
    branch_k, branch_v = branch_keys[0], branch_values[0]
    seq_index = lax.axis_index("seq")
    head_index = lax.axis_index("head")
    places = jnp.repeat(answer_positions[0], heads_here)
    place_column = places[:, None]
    place_row = jnp.tile(places, heads)[None, :]
    swap_heads = [(i, (i + 1) % heads) for i in range(heads)]
    shifts = [[(i, (i + m) % branches) for i in range(branches)] for m in range(1, branches)]

    gathered = jnp.concatenate([queries.reshape(rows, width), output_cotangent.reshape(rows, width)], 0)
    for bit in lay.bits:
        pairs = [(i, i ^ (1 << bit)) for i in range(count)]
        gathered = jnp.concatenate([gathered, lax.ppermute(gathered, "seq", pairs)], 0)
    other = lax.ppermute(gathered, "head", swap_heads)

    message_rows = 3 * rows + 8 * tiles
    if lay.swap:
        message_shapes = [((message_rows, width), bf16)] * (count - 1)
    else:
        message_shapes = [((count, message_rows, width), bf16)]
    own, coded, *messages = call(
        forward_kernel, lay,
        (gathered, root_keys, root_values, branch_k, branch_v, place_column),
        [((3 * rows, width), f32), ((8, tiles * LANES), f32)] + message_shapes,
        [pltpu.VMEM((3, total, width), f32), pltpu.VMEM((total, width), bf16),
         pltpu.VMEM((total, width), bf16)])
    if lay.swap:
        received = [lax.ppermute(message, "seq", [(i, i ^ (m + 1)) for i in range(count)])
                    for m, message in enumerate(messages)]
    else:
        whole = lax.all_to_all(messages[0], "seq", split_axis=0, concat_axis=0, tiled=True)
        received = [lax.dynamic_index_in_dim(whole, seq_index ^ m, 0, keepdims=False)
                    for m in range(1, count)]

    pair = jnp.concatenate([gathered, other], 0)
    far = [lax.ppermute(pair, "branch", s) for s in shifts]

    def weights_shapes(keys):
        shapes = [((keys, lanes), bf16), ((keys, lanes), bf16), ((8, lanes), f32),
                  ((lanes, width), bf16), ((lanes, width), bf16)]
        wide = cut(lanes, 384)[0][1]
        return shapes, [pltpu.VMEM((keys, wide), f32), pltpu.VMEM((keys, wide), f32)]

    shapes, scratch = weights_shapes(branch_count + root_count)
    own_pre = call(own_pre_kernel, lay,
                   (gathered, other, place_row, root_keys, root_values, branch_k, branch_v),
                   shapes, scratch)

    tall = -(-2 * count // 8) * 8
    final, every = call(combine_kernel, lay, (coded, *received),
                        [((8, tiles * LANES), f32), ((tall, tiles * LANES), f32)])
    other_final = lax.ppermute(final, "head", swap_heads)
    a, b = final[:, :total], other_final[:, :total]
    stats = jnp.where(head_index == 0, jnp.concatenate([a, b], 1), jnp.concatenate([b, a], 1))
    far_stats = [lax.ppermute(stats, "branch", s) for s in shifts]

    def final_scratch(keys):
        blocks = -(-keys // 256)
        return ([pltpu.VMEM((lanes, 2 * width), bf16), pltpu.VMEM((lanes, width), bf16)],
                [pltpu.VMEM((keys, width), f32), pltpu.VMEM((keys, width), f32),
                 pltpu.SemaphoreType.DMA((3, max(2, blocks)))])

    first, last = final_scratch(branch_count)
    sums = ((root_count, width), f32)
    acc_k, acc_v, attention, query_grad, branch_gk, branch_gv = call(
        own_final_kernel, lay, (*own_pre, stats, own, every, *received),
        [sums, sums, ((answers_here, heads_here, width), bf16),
         ((answers_here, heads_here, width), f32),
         ((branch_count, width), f32), ((branch_count, width), f32)],
        first + [pltpu.VMEM((tiles * LANES, LANES), f32),
                 pltpu.VMEM((answers_here, heads_here, width), bf16),
                 pltpu.VMEM((answers_here, heads_here, width), f32)] + last, away=4)
    shapes, scratch = weights_shapes(root_count)
    first, last = final_scratch(root_count)
    for pair, pair_stats in zip(far, far_stats):
        pre = call(other_pre_kernel, lay, (pair, root_keys, root_values),
                   shapes, scratch)
        acc_k, acc_v = call(other_final_kernel, lay, (*pre, pair_stats, acc_k, acc_v),
                            [sums, sums], first + last, away=2)
    return (attention[None], query_grad[None], acc_k, acc_v, branch_gk[None], branch_gv[None])


def solution(mesh):
    rows = P(("parts", "branch"), "seq", "head", None)
    root = P(("parts", "seq"), None)
    branch = P(("parts", "branch"), "seq", None)
    return jax.shard_map(
        functools.partial(per_device, mesh),
        mesh=mesh,
        in_specs=(rows, rows, root, root, branch, branch, P(("parts", "branch"), None)),
        out_specs=(rows, rows, root, root, branch, branch),
        check_vma=False,
    )
```

profile of v0, /device:TPU:0, one launch (start us, length us, event | category | flops | bytes accessed | tf_op | source)
XLA Modules:
  0.0 33.8 jit_solution(7717411208609984691)
XLA Ops:
  0.6 0.0 copy-start.5
  0.6 0.8 %pad_maximum_fusion.2 = bf16[96,128]{1,0:T(8,128)(2,1)S(1)} fusion(bf16[48,128]{1,0:T(8,128)(2,1)} %bitcast.16, bf16[48,128]{1,0:T(8,128)(2,1)} %bitcast.20), kind=kLoop, calls=%fused_computation.2 | loop fusion | flops 49152 | bytes 49152 | tf_op jit(solution)/shard_map/concatenate | solution.py:359
  1.4 0.0 copy-start.4
  1.4 4.1 %collective-permute-start = (bf16[96,128]{1,0:T(8,128)(2,1)S(1)}, bf16[96,128]{1,0:T(8,128)(2,1)S(1)}, u32[]{:S(2)}, u32[]{:S(2)}) collective-permute-start(bf16[96,128]{1,0:T(8,128)(2,1)S(1)} %pad_maximum_fusion.2), channel_id=1, source_target_pairs={{0,4},{2,6},{4,0},{6,2},{1,5},{3,7},{5,1},{7,3},{8,12},{10,14},{12... | collective-permute-start | bytes 73736 | tf_op jit(solution)/shard_map/ppermute | solution.py:362
  5.5 0.0 copy-done.5
  5.5 0.0 copy-done.4
  5.5 1.8 %collective-permute-done = bf16[96,128]{1,0:T(8,128)(2,1)S(1)} collective-permute-done((bf16[96,128]{1,0:T(8,128)(2,1)S(1)}, bf16[96,128]{1,0:T(8,128)(2,1)S(1)}, u32[]{:S(2)}, u32[]{:S(2)}) %collective-permute-start) | collective-permute-done | bytes 24608 | tf_op jit(solution)/shard_map/ppermute | solution.py:362
  7.3 1.9 %collective-permute-start.1 = (bf16[192,128]{1,0:T(8,128)(2,1)S(1)}, bf16[192,128]{1,0:T(8,128)(2,1)S(1)}, u32[]{:S(2)}, u32[]{:S(2)}) collective-permute-start(bf16[192,128]{1,0:T(8,128)(2,1)S(1)} %pad_maximum_fusion.1), channel_id=1, source_target_pairs={{0,2},{2,0},{4,6},{6,4},{1,3},{3,1},{5,7},{7,5},{8,10},{10,8},{12,... | collective-permute-start | bytes 147464 | tf_op jit(solution)/shard_map/ppermute | solution.py:362
  9.2 2.2 %collective-permute-done.1 = bf16[192,128]{1,0:T(8,128)(2,1)S(1)} collective-permute-done((bf16[192,128]{1,0:T(8,128)(2,1)S(1)}, bf16[192,128]{1,0:T(8,128)(2,1)S(1)}, u32[]{:S(2)}, u32[]{:S(2)}) %collective-permute-start.1) | collective-permute-done | bytes 49184 | tf_op jit(solution)/shard_map/ppermute | solution.py:362
  11.4 0.0 copy-start.3
  11.4 0.1 collective-permute-start.2
  11.5 0.0 copy-start.6
  11.5 0.0 copy-start.2
  11.5 0.0 copy-start
  11.5 0.0 copy-start.1
  11.6 1.2 %collective-permute-done.2.other = bf16[384,128]{1,0:T(8,128)(2,1)S(1)} collective-permute-done((bf16[384,128]{1,0:T(8,128)(2,1)S(1)}, bf16[384,128]{1,0:T(8,128)(2,1)S(1)}, u32[]{:S(2)}, u32[]{:S(2)}) %collective-permute-start.2) | collective-permute-done | bytes 98336 | tf_op jit(solution)/shard_map/ppermute | solution.py:363
  12.8 2.0 %collective-permute-start.7 = (bf16[768,128]{1,0:T(8,128)(2,1)S(1)}, bf16[768,128]{1,0:T(8,128)(2,1)S(1)}, u32[]{:S(2)}, u32[]{:S(2)}) collective-permute-start(bf16[768,128]{1,0:T(8,128)(2,1)S(1)} %constant_dynamic-update-slice_fusion), channel_id=1, source_target_pairs={{0,8},{8,0},{1,9},{9,1},{2,10},{10,2},{3,11},{11,3},{4,12},{12,4},... | collective-permute-start | bytes 589832 | tf_op jit(solution)/shard_map/ppermute | solution.py:385
  14.8 0.0 copy-done.6
  14.8 0.1 broadcast_in_dim.15
  14.9 0.1 broadcast_in_dim_reshape.4.places
  15.0 0.0 copy-done.3
  15.0 0.0 copy-done.2
  15.0 0.0 copy-done
  15.0 0.0 copy-done.1
  15.0 1.0 %shard_map.119 = (f32[144,128]{1,0:T(8,128)S(1)}, f32[8,256]{1,0:T(8,128)S(1)}, bf16[160,128]{1,0:T(8,128)(2,1)S(1)}, bf16[160,128]{1,0:T(8,128)(2,1)S(1)}, bf16[160,128]{1,0:T(8,128)(2,1)S(1)}) custom-call(bf16[384,128]{1,0:T(8,128)(2,1)S(1)} %pad_maximum_fusion.mine.gathered, bf16[512,128]{1,0:T(8,128)(2,1)S(1)} %copy-done, ...), custom_call_target="tpu_custom_call" | custom-call | tf_op jit(solution)/shard_map/pallas_call | solution.py:326
  16.0 1.5 %collective-permute-start.3 = (bf16[160,128]{1,0:T(8,128)(2,1)S(1)}, bf16[160,128]{1,0:T(8,128)(2,1)S(1)}, u32[]{:S(2)}, u32[]{:S(2)}) collective-permute-start(bf16[160,128]{1,0:T(8,128)(2,1)S(1)} %get-tuple-element.37), channel_id=1, source_target_pairs={{0,2},{2,0},{4,6},{6,4},{1,3},{3,1},{5,7},{7,5},{8,10},{10,8},{12,... | collective-permute-start | bytes 122888 | tf_op jit(solution)/shard_map/ppermute | solution.py:377
  17.5 2.8 %collective-permute-start.4 = (bf16[160,128]{1,0:T(8,128)(2,1)S(1)}, bf16[160,128]{1,0:T(8,128)(2,1)S(1)}, u32[]{:S(2)}, u32[]{:S(2)}) collective-permute-start(bf16[160,128]{1,0:T(8,128)(2,1)S(1)} %get-tuple-element.38), channel_id=1, source_target_pairs={{0,4},{2,6},{4,0},{6,2},{1,5},{3,7},{5,1},{7,3},{8,12},{10,14},{12... | collective-permute-start | bytes 122888 | tf_op jit(solution)/shard_map/ppermute | solution.py:377
  20.2 0.2 collective-permute-start.5
  20.4 0.0 collective-permute-done.3.rest_0_
  20.4 2.8 %collective-permute-done.4.rest_1_ = bf16[160,128]{1,0:T(8,128)(2,1)S(1)} collective-permute-done((bf16[160,128]{1,0:T(8,128)(2,1)S(1)}, bf16[160,128]{1,0:T(8,128)(2,1)S(1)}, u32[]{:S(2)}, u32[]{:S(2)}) %collective-permute-start.4) | collective-permute-done | bytes 40992 | tf_op jit(solution)/shard_map/ppermute | solution.py:377
  23.2 2.8 %collective-permute-done.5.rest_2_ = bf16[160,128]{1,0:T(8,128)(2,1)S(1)} collective-permute-done((bf16[160,128]{1,0:T(8,128)(2,1)S(1)}, bf16[160,128]{1,0:T(8,128)(2,1)S(1)}, u32[]{:S(2)}, u32[]{:S(2)}) %collective-permute-start.5) | collective-permute-done | bytes 40992 | tf_op jit(solution)/shard_map/ppermute | solution.py:377
  26.1 0.1 collective-permute-start.6
  26.1 1.2 %collective-permute-done.6 = f32[8,256]{1,0:T(8,128)S(1)} collective-permute-done((f32[8,256]{1,0:T(8,128)S(1)}, f32[8,256]{1,0:T(8,128)S(1)}, u32[]{:S(2)}, u32[]{:S(2)}) %collective-permute-start.6) | collective-permute-done | bytes 8224 | tf_op jit(solution)/shard_map/ppermute | solution.py:401
  27.3 0.1 maximum_select_fusion.stats
  27.4 0.5 %collective-permute-start.8 = (f32[8,384]{1,0:T(8,128)S(1)}, f32[8,384]{1,0:T(8,128)S(1)}, u32[]{:S(2)}, u32[]{:S(2)}) collective-permute-start(f32[8,384]{1,0:T(8,128)S(1)} %maximum_select_fusion.stats), channel_id=1, source_target_pairs={{0,8},{8,0},{1,9},{9,1},{2,10},{10,2},{3,11},{11,3},{4,12},{12,4},... | collective-permute-start | bytes 36872 | tf_op jit(solution)/shard_map/ppermute | solution.py:404
  27.9 0.1 tile.7
  28.0 0.1 broadcast_in_dim_tile.3.places
  28.1 1.1 %shard_map.118 = (bf16[1024,384]{1,0:T(8,128)(2,1)S(1)}, bf16[1024,384]{1,0:T(8,128)(2,1)S(1)}, f32[8,384]{1,0:T(8,128)S(1)}, bf16[384,128]{1,0:T(8,128)(2,1)S(1)}, bf16[384,128]{1,0:T(8,128)(2,1)S(1)}) custom-call(bf16[384,128]{1,0:T(8,128)(2,1)S(1)} %pad_maximum_fusion.mine.gathered, bf16[384,128]{1,0:T(8,128)(2,1)S(1)} %collective-permute-done.2.other, ...), custom_call_target="tpu_custom_call" | custom-call | tf_op jit(solution)/shard_map/pallas_call | solution.py:326
  29.2 2.3 %shard_map.121 = (f32[512,128]{1,0:T(8,128)S(1)}, f32[512,128]{1,0:T(8,128)S(1)}, bf16[12,4,128]{2,1,0:T(4,128)(2,1)}, f32[12,4,128]{2,1,0:T(4,128)}, f32[512,128]{1,0:T(8,128)}, /*index=5*/f32[512,128]{1,0:T(8,128)}) custom-call(bf16[1024,384]{1,0:T(8,128)(2,1)S(1)} %get-tuple-element.31.probs, bf16[1024,384]{1,0:T(8,128)(2,1)S(1)} %get-tuple-element.32.slopes, ...), custom_call_target="tpu_custom_call" | custom-call | tf_op jit(solution)/shard_map/pallas_call | solution.py:326
  31.5 0.0 collective-permute-done.7.pair
  31.5 0.7 %shard_map.122 = (bf16[512,384]{1,0:T(8,128)(2,1)S(1)}, bf16[512,384]{1,0:T(8,128)(2,1)S(1)}, f32[8,384]{1,0:T(8,128)S(1)}, bf16[384,128]{1,0:T(8,128)(2,1)S(1)}, bf16[384,128]{1,0:T(8,128)(2,1)S(1)}) custom-call(bf16[768,128]{1,0:T(8,128)(2,1)S(1)} %collective-permute-done.7.pair, bf16[512,128]{1,0:T(8,128)(2,1)S(1)} %copy-done, bf16[512,128]{1,0:T(8,128)(2,1)S(1)} %copy-done.1), custom_call_target="tpu_custom_call" | custom-call | tf_op jit(solution)/shard_map/pallas_call | solution.py:326
  32.2 0.0 collective-permute-done.8.stats
  32.2 1.6 %shard_map.123 = (f32[512,128]{1,0:T(8,128)}, f32[512,128]{1,0:T(8,128)}) custom-call(bf16[512,384]{1,0:T(8,128)(2,1)S(1)} %get-tuple-element.45.probs, bf16[512,384]{1,0:T(8,128)(2,1)S(1)} %get-tuple-element.46.slopes, f32[8,384]{1,0:T(8,128)S(1)} %get-tuple-element.47.local, bf16[384,128]{1,0:T(8,128)(2,1)S(1)} %get-tuple-element.48.query, ...), custom_call_target="tpu_custom_call" | custom-call | tf_op jit(solution)/shard_map/pallas_call | solution.py:326
  (9 shorter events, 0.1 us)
Async XLA Ops:
  0.6 4.9 %copy-start.5 = (bf16[1,12,4,128]{3,2,1,0:T(4,128)(2,1)S(1)}, bf16[1,12,4,128]{3,2,1,0:T(4,128)(2,1)}, u32[]{:S(2)}) copy-start(bf16[1,12,4,128]{3,2,1,0:T(4,128)(2,1)} %param.7) | copy-start | bytes 36868
  1.4 4.1 %copy-start.4 = (bf16[1,12,4,128]{3,2,1,0:T(4,128)(2,1)S(1)}, bf16[1,12,4,128]{3,2,1,0:T(4,128)(2,1)}, u32[]{:S(2)}) copy-start(bf16[1,12,4,128]{3,2,1,0:T(4,128)(2,1)} %param.8) | copy-start | bytes 36868
  1.4 5.9 %collective-permute-start = (bf16[96,128]{1,0:T(8,128)(2,1)S(1)}, bf16[96,128]{1,0:T(8,128)(2,1)S(1)}, u32[]{:S(2)}, u32[]{:S(2)}) collective-permute-start(bf16[96,128]{1,0:T(8,128)(2,1)S(1)} %pad_maximum_fusion.2), channel_id=1, source_target_pairs={{0,4},{2,6},{4,0},{6,2},{1,5},{3,7},{5,1},{7,3},{8,12},{10,14},{12... | collective-permute-start | bytes 73736 | tf_op jit(solution)/shard_map/ppermute | solution.py:362
  7.3 4.1 %collective-permute-start.1 = (bf16[192,128]{1,0:T(8,128)(2,1)S(1)}, bf16[192,128]{1,0:T(8,128)(2,1)S(1)}, u32[]{:S(2)}, u32[]{:S(2)}) collective-permute-start(bf16[192,128]{1,0:T(8,128)(2,1)S(1)} %pad_maximum_fusion.1), channel_id=1, source_target_pairs={{0,2},{2,0},{4,6},{6,4},{1,3},{3,1},{5,7},{7,5},{8,10},{10,8},{12,... | collective-permute-start | bytes 147464 | tf_op jit(solution)/shard_map/ppermute | solution.py:362
  11.4 3.6 %copy-start.3 = (bf16[1,512,128]{2,1,0:T(8,128)(2,1)S(1)}, bf16[1,512,128]{2,1,0:T(8,128)(2,1)}, u32[]{:S(2)}) copy-start(bf16[1,512,128]{2,1,0:T(8,128)(2,1)} %param.12) | copy-start | bytes 393220
  11.4 1.4 %collective-permute-start.2 = (bf16[384,128]{1,0:T(8,128)(2,1)S(1)}, bf16[384,128]{1,0:T(8,128)(2,1)S(1)}, u32[]{:S(2)}, u32[]{:S(2)}) collective-permute-start(bf16[384,128]{1,0:T(8,128)(2,1)S(1)} %pad_maximum_fusion.mine.gathered), channel_id=1, source_target_pairs={{0,1},{1,0},{2,3},{3,2},{4,5},{5,4},{6,7},{7,6},{8,9},{9,8},{10,11... | collective-permute-start | bytes 294920 | tf_op jit(solution)/shard_map/ppermute | solution.py:363
  11.5 3.3 %copy-start.6 = (s32[1,48]{1,0:T(1,128)S(1)}, s32[1,48]{1,0:T(1,128)}, u32[]{:S(2)}) copy-start(s32[1,48]{1,0:T(1,128)} %param.13) | copy-start | bytes 580
  11.5 3.5 %copy-start.2 = (bf16[1,512,128]{2,1,0:T(8,128)(2,1)S(1)}, bf16[1,512,128]{2,1,0:T(8,128)(2,1)}, u32[]{:S(2)}) copy-start(bf16[1,512,128]{2,1,0:T(8,128)(2,1)} %param.11) | copy-start | bytes 393220
  11.5 3.5 %copy-start = (bf16[512,128]{1,0:T(8,128)(2,1)S(1)}, bf16[512,128]{1,0:T(8,128)(2,1)}, u32[]{:S(2)}) copy-start(bf16[512,128]{1,0:T(8,128)(2,1)} %root_k.5) | copy-start | bytes 393220
  11.5 3.5 %copy-start.1 = (bf16[512,128]{1,0:T(8,128)(2,1)S(1)}, bf16[512,128]{1,0:T(8,128)(2,1)}, u32[]{:S(2)}) copy-start(bf16[512,128]{1,0:T(8,128)(2,1)} %root_v.5) | copy-start | bytes 393220
  12.8 18.7 %collective-permute-start.7 = (bf16[768,128]{1,0:T(8,128)(2,1)S(1)}, bf16[768,128]{1,0:T(8,128)(2,1)S(1)}, u32[]{:S(2)}, u32[]{:S(2)}) collective-permute-start(bf16[768,128]{1,0:T(8,128)(2,1)S(1)} %constant_dynamic-update-slice_fusion), channel_id=1, source_target_pairs={{0,8},{8,0},{1,9},{9,1},{2,10},{10,2},{3,11},{11,3},{4,12},{12,4},... | collective-permute-start | bytes 589832 | tf_op jit(solution)/shard_map/ppermute | solution.py:385
  16.0 4.5 %collective-permute-start.3 = (bf16[160,128]{1,0:T(8,128)(2,1)S(1)}, bf16[160,128]{1,0:T(8,128)(2,1)S(1)}, u32[]{:S(2)}, u32[]{:S(2)}) collective-permute-start(bf16[160,128]{1,0:T(8,128)(2,1)S(1)} %get-tuple-element.37), channel_id=1, source_target_pairs={{0,2},{2,0},{4,6},{6,4},{1,3},{3,1},{5,7},{7,5},{8,10},{10,8},{12,... | collective-permute-start | bytes 122888 | tf_op jit(solution)/shard_map/ppermute | solution.py:377
  17.5 5.8 %collective-permute-start.4 = (bf16[160,128]{1,0:T(8,128)(2,1)S(1)}, bf16[160,128]{1,0:T(8,128)(2,1)S(1)}, u32[]{:S(2)}, u32[]{:S(2)}) collective-permute-start(bf16[160,128]{1,0:T(8,128)(2,1)S(1)} %get-tuple-element.38), channel_id=1, source_target_pairs={{0,4},{2,6},{4,0},{6,2},{1,5},{3,7},{5,1},{7,3},{8,12},{10,14},{12... | collective-permute-start | bytes 122888 | tf_op jit(solution)/shard_map/ppermute | solution.py:377
  20.2 5.8 %collective-permute-start.5 = (bf16[160,128]{1,0:T(8,128)(2,1)S(1)}, bf16[160,128]{1,0:T(8,128)(2,1)S(1)}, u32[]{:S(2)}, u32[]{:S(2)}) collective-permute-start(bf16[160,128]{1,0:T(8,128)(2,1)S(1)} %get-tuple-element.39), channel_id=1, source_target_pairs={{0,6},{2,4},{4,2},{6,0},{1,7},{3,5},{5,3},{7,1},{8,14},{10,12},{12... | collective-permute-start | bytes 122888 | tf_op jit(solution)/shard_map/ppermute | solution.py:377
  26.1 1.2 %collective-permute-start.6 = (f32[8,256]{1,0:T(8,128)S(1)}, f32[8,256]{1,0:T(8,128)S(1)}, u32[]{:S(2)}, u32[]{:S(2)}) collective-permute-start(f32[8,256]{1,0:T(8,128)S(1)} %get-tuple-element.40), channel_id=1, source_target_pairs={{0,1},{1,0},{2,3},{3,2},{4,5},{5,4},{6,7},{7,6},{8,9},{9,8},{10,11... | collective-permute-start | bytes 24584 | tf_op jit(solution)/shard_map/ppermute | solution.py:401
  27.4 4.8 %collective-permute-start.8 = (f32[8,384]{1,0:T(8,128)S(1)}, f32[8,384]{1,0:T(8,128)S(1)}, u32[]{:S(2)}, u32[]{:S(2)}) collective-permute-start(f32[8,384]{1,0:T(8,128)S(1)} %maximum_select_fusion.stats), channel_id=1, source_target_pairs={{0,8},{8,0},{1,9},{9,1},{2,10},{10,2},{3,11},{11,3},{4,12},{12,4},... | collective-permute-start | bytes 36872 | tf_op jit(solution)/shard_map/ppermute | solution.py:404
where the time goes:
time: 34 us; the launch traced here: 33.8 us
  starting transfers between devices  13.1 us (39%)
  waiting for transfers between devices  12 us (35%)
  Pallas kernels  6.65 us (20%)
  other arithmetic  0.86 us (3%)
  between operations  0.81 us (2%)
  local copies, waits for them, and re-layouts  0.42 us (1%)
    pallas_call x6, Pallas kernels, call(): pl.pallas_call(functools.partial(kernel, lay=lay), out_shape=[jax.ShapeDt...  6.65 us
    ppermute x2, starting transfers between devices, body(): lax.ppermute(gathered, 'seq', pairs)  5.96 us
    ppermute x3, waiting for transfers between devices, body(): lax.ppermute(message, 'seq', [(i, i ^ m + 1) for i in range(count)])  5.6 us
    ppermute x3, starting transfers between devices, body(): lax.ppermute(message, 'seq', [(i, i ^ m + 1) for i in range(count)])  4.45 us
    ppermute x2, waiting for transfers between devices, body(): lax.ppermute(gathered, 'seq', pairs)  3.98 us
    ppermute x1, starting transfers between devices, body(): far = [lax.ppermute(pair, 'branch', s) for s in shifts]  2.02 us
    ppermute x1, waiting for transfers between devices, body(): other = lax.ppermute(gathered, 'head', swap_heads)  1.22 us
    ppermute x1, waiting for transfers between devices, body(): other_final = lax.ppermute(final, 'head', swap_heads)  1.15 us
  transfers between devices with their start and end apart: 9, of which 6 were waited for; matrix products, arithmetic and copies ran while one was open for 1% of the time, Pallas kernels for 15%

commit v1 on v0

--- a/solution.py
+++ b/solution.py
@@ -11,6 +11,9 @@
 NEG = -1e30
 LOG2E = math.log2(math.e)
 LANES = 128
+SEQ_FLIPS = (0, 1, 1, 0)
+FAR_FLIP = 1
+STAT_FLIP = 1
 
 bf16 = jnp.bfloat16
 f32 = jnp.float32
@@ -206,7 +209,7 @@
 
 def other_pre_kernel(pair, root_k, root_v, probs, slopes, local, query, grad,
                      logits, products, *, lay):
-    place, half = lax.axis_index("seq"), lax.axis_index("head")
+    place, half = lax.axis_index("seq"), lax.axis_index("head") ^ FAR_FLIP
     arrange(place, pair, 0, query, grad, half * lay.total, lay)
     arrange(place, pair, 2 * lay.total, query, grad, (1 - half) * lay.total, lay)
     local_weights([(0, root_k, root_v, None)], query, grad, probs, slopes, local, 2,
@@ -232,17 +235,9 @@
     return wide[:, LANES:] + nn(slopes[spot, :], single[...]), wide[:, 0:LANES]
 
 
-def own_final_kernel(probs, slopes, local, query, grad, stats, own, every, *rest, lay):
-    messages = rest[:lay.count - 1]
-    (acc_k, acc_v, out_a, out_q, out_k, out_v, both, single, columns,
-     hold_a, hold_q, hold_k, hold_v, sems) = rest[lay.count - 1:]
+def finish_kernel(own, every, *rest, lay):
+    messages, (out_a, out_q, columns) = rest[:-3], rest[-3:]
     rows, count = lay.rows, lay.count
-    copies = []
-
-    def send(source, target, sem):
-        copies.append(pltpu.make_async_copy(source, target, sem))
-        copies[-1].start()
-
     tall = every.shape[0]
     for k in range(lay.tiles):
         piece = every[:, k * LANES:(k + 1) * LANES]
@@ -266,43 +261,46 @@
         b_part = source[2 * rows:3 * rows, :].astype(f32)
         attended = attended + shares[v] * o_part
         slope_sum = slope_sum + shares[v] * (a_part + (deltas[v] - delta) * b_part)
-    hold_a[...] = attended.reshape(out_a.shape).astype(bf16)
-    send(hold_a, out_a, sems.at[2, 0])
-    hold_q[...] = (slope_sum * lay.scale).reshape(out_q.shape)
-    send(hold_q, out_q, sems.at[2, 1])
-
-    branch_count = hold_k.shape[0]
+    out_a[...] = attended.reshape(out_a.shape).astype(bf16)
+    out_q[...] = (slope_sum * lay.scale).reshape(out_q.shape)
+
+
+def own_final_kernel(probs, slopes, local, query, grad, stats,
+                     acc_k, acc_v, branch_k, branch_v, both, single, *, lay):
+    count = branch_k.shape[0]
     block = 256
-    scaled_rows(local, 0, stats, query, grad, both, single, lay.scale)
-    for n, at in enumerate(range(0, branch_count, block)):
-        spot = slice(at, min(at + block, branch_count))
-        hold_k[spot, :], hold_v[spot, :] = gradients(probs, slopes, spot, both, single)
-        send(hold_k.at[spot, :], out_k.at[spot, :], sems.at[0, n])
-        send(hold_v.at[spot, :], out_v.at[spot, :], sems.at[1, n])
-    scaled_rows(local, 2, stats, query, grad, both, single, lay.scale)
-    for at in range(0, acc_k.shape[0], block):
-        size = min(block, acc_k.shape[0] - at)
-        acc_k[at:at + size, :], acc_v[at:at + size, :] = gradients(
-            probs, slopes, slice(branch_count + at, branch_count + at + size), both, single)
-    for copy in copies:
-        copy.wait()
-
-
-def other_final_kernel(probs, slopes, local, query, grad, stats, acc_k, acc_v, out_k, out_v,
+    for base, line, to_k, to_v in ((0, 0, branch_k, branch_v), (count, 2, acc_k, acc_v)):
+        scaled_rows(local, line, stats, query, grad, both, single, lay.scale)
+        for at in range(0, to_k.shape[0], block):
+            size = min(block, to_k.shape[0] - at)
+            to_k[at:at + size, :], to_v[at:at + size, :] = gradients(
+                probs, slopes, slice(base + at, base + at + size), both, single)
+
+
+def other_final_kernel(probs, slopes, local, query, grad, stats, acc_k, acc_v,
+                       branch_k, branch_v, attended, query_grad,
+                       out_k, out_v, out_bk, out_bv, out_a, out_q,
                        both, single, hold_k, hold_v, sems, *, lay):
+    copies = []
+
+    def send(source, target, sem):
+        copies.append(pltpu.make_async_copy(source, target, sem))
+        copies[-1].start()
+
+    send(branch_k, out_bk, sems.at[2, 0])
+    send(branch_v, out_bv, sems.at[2, 1])
+    send(attended, out_a, sems.at[3, 0])
+    send(query_grad, out_q, sems.at[3, 1])
     scaled_rows(local, 2, stats, query, grad, both, single, lay.scale)
     count = hold_k.shape[0]
-    copies = []
     block = 256
     for n, at in enumerate(range(0, count, block)):
         spot = slice(at, min(at + block, count))
         more_k, more_v = gradients(probs, slopes, spot, both, single)
         hold_k[spot, :] = acc_k[spot, :] + more_k
-        copies.append(pltpu.make_async_copy(hold_k.at[spot, :], out_k.at[spot, :], sems.at[0, n]))
-        copies[-1].start()
+        send(hold_k.at[spot, :], out_k.at[spot, :], sems.at[0, n])
         hold_v[spot, :] = acc_v[spot, :] + more_v
-        copies.append(pltpu.make_async_copy(hold_v.at[spot, :], out_v.at[spot, :], sems.at[1, n]))
-        copies[-1].start()
+        send(hold_v.at[spot, :], out_v.at[spot, :], sems.at[1, n])
     for copy in copies:
         copy.wait()
 
@@ -329,6 +327,10 @@
         in_specs=[VMEM] * len(args), out_specs=specs, scratch_shapes=list(scratch),
         compiler_params=pltpu.CompilerParams(vmem_limit_bytes=limit),
     )(*args)
+
+
+def move(value, axis, pairs):
+    return lax.ppermute(value, axis, pairs)
 
 
 def per_device(mesh, queries, output_cotangent, root_keys, root_values,
@@ -353,14 +355,24 @@
     places = jnp.repeat(answer_positions[0], heads_here)
     place_column = places[:, None]
     place_row = jnp.tile(places, heads)[None, :]
+    crossing = lay.swap and heads == 2
+
+    def seq_pairs(m):
+        flip = SEQ_FLIPS[m] if crossing else 0
+        return [(z * heads + c, (z ^ m) * heads + (c ^ flip)) for z in range(count) for c in range(heads)]
+
+    def far_pairs(m, flip):
+        return [(b * heads + c, (b + m) % branches * heads + (c ^ flip))
+                for b in range(branches) for c in range(heads)]
+
     swap_heads = [(i, (i + 1) % heads) for i in range(heads)]
-    shifts = [[(i, (i + m) % branches) for i in range(branches)] for m in range(1, branches)]
+    shifts = range(1, branches)
 
     gathered = jnp.concatenate([queries.reshape(rows, width), output_cotangent.reshape(rows, width)], 0)
     for bit in lay.bits:
-        pairs = [(i, i ^ (1 << bit)) for i in range(count)]
-        gathered = jnp.concatenate([gathered, lax.ppermute(gathered, "seq", pairs)], 0)
-    other = lax.ppermute(gathered, "head", swap_heads)
+        pairs = seq_pairs(1 << bit)
+        gathered = jnp.concatenate([gathered, move(gathered, ("seq", "head"), pairs)], 0)
+    other = move(gathered, "head", swap_heads)
 
     message_rows = 3 * rows + 8 * tiles
     if lay.swap:
@@ -374,7 +386,7 @@
         [pltpu.VMEM((3, total, width), f32), pltpu.VMEM((total, width), bf16),
          pltpu.VMEM((total, width), bf16)])
     if lay.swap:
-        received = [lax.ppermute(message, "seq", [(i, i ^ (m + 1)) for i in range(count)])
+        received = [move(message, ("seq", "head"), seq_pairs(m + 1))
                     for m, message in enumerate(messages)]
     else:
         whole = lax.all_to_all(messages[0], "seq", split_axis=0, concat_axis=0, tiled=True)
@@ -382,7 +394,7 @@
                     for m in range(1, count)]
 
     pair = jnp.concatenate([gathered, other], 0)
-    far = [lax.ppermute(pair, "branch", s) for s in shifts]
+    far = [move(pair, ("branch", "head"), far_pairs(m, FAR_FLIP if heads == 2 else 0)) for m in shifts]
 
     def weights_shapes(keys):
         shapes = [((keys, lanes), bf16), ((keys, lanes), bf16), ((8, lanes), f32),
@@ -398,34 +410,34 @@
     tall = -(-2 * count // 8) * 8
     final, every = call(combine_kernel, lay, (coded, *received),
                         [((8, tiles * LANES), f32), ((tall, tiles * LANES), f32)])
-    other_final = lax.ppermute(final, "head", swap_heads)
+    other_final = move(final, "head", swap_heads)
     a, b = final[:, :total], other_final[:, :total]
     stats = jnp.where(head_index == 0, jnp.concatenate([a, b], 1), jnp.concatenate([b, a], 1))
-    far_stats = [lax.ppermute(stats, "branch", s) for s in shifts]
+    far_stats = [move(stats, ("branch", "head"), far_pairs(m, STAT_FLIP if heads == 2 else 0)) for m in shifts]
 
     def final_scratch(keys):
         blocks = -(-keys // 256)
         return ([pltpu.VMEM((lanes, 2 * width), bf16), pltpu.VMEM((lanes, width), bf16)],
                 [pltpu.VMEM((keys, width), f32), pltpu.VMEM((keys, width), f32),
-                 pltpu.SemaphoreType.DMA((3, max(2, blocks)))])
-
-    first, last = final_scratch(branch_count)
-    sums = ((root_count, width), f32)
-    acc_k, acc_v, attention, query_grad, branch_gk, branch_gv = call(
-        own_final_kernel, lay, (*own_pre, stats, own, every, *received),
-        [sums, sums, ((answers_here, heads_here, width), bf16),
-         ((answers_here, heads_here, width), f32),
-         ((branch_count, width), f32), ((branch_count, width), f32)],
-        first + [pltpu.VMEM((tiles * LANES, LANES), f32),
-                 pltpu.VMEM((answers_here, heads_here, width), bf16),
-                 pltpu.VMEM((answers_here, heads_here, width), f32)] + last, away=4)
+                 pltpu.SemaphoreType.DMA((4, max(2, blocks)))])
+
+    row_shapes = [((answers_here, heads_here, width), bf16), ((answers_here, heads_here, width), f32)]
+    attention, query_grad = call(
+        finish_kernel, lay, (own, every, *received),
+        row_shapes, [pltpu.VMEM((tiles * LANES, LANES), f32)])
+    root_sum, branch_sum = ((root_count, width), f32), ((branch_count, width), f32)
+    first, last = final_scratch(root_count)
+    acc_k, acc_v, branch_gk, branch_gv = call(
+        own_final_kernel, lay, (*own_pre, stats),
+        [root_sum, root_sum, branch_sum, branch_sum], first)
     shapes, scratch = weights_shapes(root_count)
-    first, last = final_scratch(root_count)
     for pair, pair_stats in zip(far, far_stats):
         pre = call(other_pre_kernel, lay, (pair, root_keys, root_values),
                    shapes, scratch)
-        acc_k, acc_v = call(other_final_kernel, lay, (*pre, pair_stats, acc_k, acc_v),
-                            [sums, sums], first + last, away=2)
+        acc_k, acc_v, branch_gk, branch_gv, attention, query_grad = call(
+            other_final_kernel, lay,
+            (*pre, pair_stats, acc_k, acc_v, branch_gk, branch_gv, attention, query_grad),
+            [root_sum, root_sum, branch_sum, branch_sum, *row_shapes], first + last, away=6)
     return (attention[None], query_grad[None], acc_k, acc_v, branch_gk[None], branch_gv[None])
 
 

time: 34 us -> 32.7 us (0.962)
  waiting for transfers between devices: 12 us -> 11.3 us
  starting transfers between devices: 13.1 us -> 12.7 us
    ppermute x9, waiting for transfers between devices: 12 us -> 11.3 us  [move(): return lax.ppermute(value, axis, pairs)]
    ppermute x9, starting transfers between devices: 13.1 us -> 12.7 us  [move(): return lax.ppermute(value, axis, pairs)]
    pallas_call x6 -> x7, Pallas kernels: 6.65 us -> 6.41 us  [call(): pl.pallas_call(functools.partial(kernel, lay=lay), out_shape=[jax.ShapeDt...]
where the time goes in v1:
time: 32.7 us; the launch traced here: 32.4 us
  starting transfers between devices  12.7 us (39%)
  waiting for transfers between devices  11.3 us (35%)
  Pallas kernels  6.41 us (20%)
  other arithmetic  0.86 us (3%)
  between operations  0.79 us (2%)
  local copies, waits for them, and re-layouts  0.41 us (1%)
    ppermute x9, starting transfers between devices, move(): return lax.ppermute(value, axis, pairs)  12.7 us
    ppermute x9, waiting for transfers between devices, move(): return lax.ppermute(value, axis, pairs)  11.3 us
    pallas_call x7, Pallas kernels, call(): pl.pallas_call(functools.partial(kernel, lay=lay), out_shape=[jax.ShapeDt...  6.41 us
    concatenate x1, other arithmetic, body(): jnp.concatenate([queries.reshape(rows, width), output_cotangent.reshape(r...  0.77 us
  transfers between devices with their start and end apart: 9, of which 6 were waited for; matrix products, arithmetic and copies ran while one was open for 1% of the time, Pallas kernels for 15%

profile of v1, /device:TPU:0, one launch (start us, length us, event | category | flops | bytes accessed | tf_op | source)
XLA Modules:
  0.0 32.4 jit_solution(5373716189539527507)
XLA Ops:
  0.6 0.0 copy-start.4
  0.6 0.8 %pad_maximum_fusion.2 = bf16[96,128]{1,0:T(8,128)(2,1)S(1)} fusion(bf16[48,128]{1,0:T(8,128)(2,1)} %bitcast.20, bf16[48,128]{1,0:T(8,128)(2,1)} %bitcast.16), kind=kLoop, calls=%fused_computation.2 | loop fusion | flops 49152 | bytes 49152 | tf_op jit(solution)/shard_map/concatenate | solution.py:371
  1.4 0.0 copy-start.5
  1.4 3.5 %collective-permute-start = (bf16[96,128]{1,0:T(8,128)(2,1)S(1)}, bf16[96,128]{1,0:T(8,128)(2,1)S(1)}, u32[]{:S(2)}, u32[]{:S(2)}) collective-permute-start(bf16[96,128]{1,0:T(8,128)(2,1)S(1)} %pad_maximum_fusion.2), channel_id=1, source_target_pairs={{0,5},{1,4},{2,7},{3,6},{4,1},{5,0},{6,3},{7,2},{8,13},{9,12},{10,... | collective-permute-start | bytes 73736 | tf_op jit(solution)/shard_map/ppermute | solution.py:333
  4.9 0.0 copy-done.4
  4.9 0.0 copy-done.5
  4.9 1.6 %collective-permute-done = bf16[96,128]{1,0:T(8,128)(2,1)S(1)} collective-permute-done((bf16[96,128]{1,0:T(8,128)(2,1)S(1)}, bf16[96,128]{1,0:T(8,128)(2,1)S(1)}, u32[]{:S(2)}, u32[]{:S(2)}) %collective-permute-start) | collective-permute-done | bytes 24608 | tf_op jit(solution)/shard_map/ppermute | solution.py:333
  6.5 1.8 %collective-permute-start.1 = (bf16[192,128]{1,0:T(8,128)(2,1)S(1)}, bf16[192,128]{1,0:T(8,128)(2,1)S(1)}, u32[]{:S(2)}, u32[]{:S(2)}) collective-permute-start(bf16[192,128]{1,0:T(8,128)(2,1)S(1)} %pad_maximum_fusion.1), channel_id=1, source_target_pairs={{0,3},{1,2},{2,1},{3,0},{4,7},{5,6},{6,5},{7,4},{8,11},{9,10},{10,... | collective-permute-start | bytes 147464 | tf_op jit(solution)/shard_map/ppermute | solution.py:333
  8.4 1.8 %collective-permute-done.1 = bf16[192,128]{1,0:T(8,128)(2,1)S(1)} collective-permute-done((bf16[192,128]{1,0:T(8,128)(2,1)S(1)}, bf16[192,128]{1,0:T(8,128)(2,1)S(1)}, u32[]{:S(2)}, u32[]{:S(2)}) %collective-permute-start.1) | collective-permute-done | bytes 49184 | tf_op jit(solution)/shard_map/ppermute | solution.py:333
  10.2 0.0 copy-start.3
  10.2 0.5 %collective-permute-start.2 = (bf16[384,128]{1,0:T(8,128)(2,1)S(1)}, bf16[384,128]{1,0:T(8,128)(2,1)S(1)}, u32[]{:S(2)}, u32[]{:S(2)}) collective-permute-start(bf16[384,128]{1,0:T(8,128)(2,1)S(1)} %pad_maximum_fusion.gathered.mine), channel_id=1, source_target_pairs={{0,1},{1,0},{2,3},{3,2},{4,5},{5,4},{6,7},{7,6},{8,9},{9,8},{10,11... | collective-permute-start | bytes 294920 | tf_op jit(solution)/shard_map/ppermute | solution.py:333
  10.7 0.0 copy-start.6
  10.7 0.0 copy-start.2
  10.7 0.0 copy-start
  10.7 0.0 copy-start.1
  10.7 0.9 %collective-permute-done.2.other = bf16[384,128]{1,0:T(8,128)(2,1)S(1)} collective-permute-done((bf16[384,128]{1,0:T(8,128)(2,1)S(1)}, bf16[384,128]{1,0:T(8,128)(2,1)S(1)}, u32[]{:S(2)}, u32[]{:S(2)}) %collective-permute-start.2) | collective-permute-done | bytes 98336 | tf_op jit(solution)/shard_map/ppermute | solution.py:333
  11.7 1.9 %collective-permute-start.3 = (bf16[768,128]{1,0:T(8,128)(2,1)S(1)}, bf16[768,128]{1,0:T(8,128)(2,1)S(1)}, u32[]{:S(2)}, u32[]{:S(2)}) collective-permute-start(bf16[768,128]{1,0:T(8,128)(2,1)S(1)} %constant_dynamic-update-slice_fusion), channel_id=1, source_target_pairs={{0,9},{1,8},{8,1},{9,0},{2,11},{3,10},{10,3},{11,2},{4,13},{5,12},... | collective-permute-start | bytes 589832 | tf_op jit(solution)/shard_map/ppermute | solution.py:333
  13.5 0.0 copy-done.6
  13.5 0.1 broadcast_in_dim.15
  13.6 0.1 broadcast_in_dim_reshape.4.places
  13.7 0.0 copy-done.3
  13.7 0.0 copy-done.2
  13.7 0.0 copy-done
  13.7 0.0 copy-done.1
  13.7 1.0 %shard_map.119 = (f32[144,128]{1,0:T(8,128)S(1)}, f32[8,256]{1,0:T(8,128)S(1)}, bf16[160,128]{1,0:T(8,128)(2,1)S(1)}, bf16[160,128]{1,0:T(8,128)(2,1)S(1)}, bf16[160,128]{1,0:T(8,128)(2,1)S(1)}) custom-call(bf16[384,128]{1,0:T(8,128)(2,1)S(1)} %pad_maximum_fusion.gathered.mine, bf16[512,128]{1,0:T(8,128)(2,1)S(1)} %copy-done, ...), custom_call_target="tpu_custom_call" | custom-call | tf_op jit(solution)/shard_map/pallas_call | solution.py:324
  14.7 1.6 %collective-permute-start.4 = (bf16[160,128]{1,0:T(8,128)(2,1)S(1)}, bf16[160,128]{1,0:T(8,128)(2,1)S(1)}, u32[]{:S(2)}, u32[]{:S(2)}) collective-permute-start(bf16[160,128]{1,0:T(8,128)(2,1)S(1)} %get-tuple-element.41), channel_id=1, source_target_pairs={{0,3},{1,2},{2,1},{3,0},{4,7},{5,6},{6,5},{7,4},{8,11},{9,10},{10,... | collective-permute-start | bytes 122888 | tf_op jit(solution)/shard_map/ppermute | solution.py:333
  16.3 3.0 %collective-permute-start.5 = (bf16[160,128]{1,0:T(8,128)(2,1)S(1)}, bf16[160,128]{1,0:T(8,128)(2,1)S(1)}, u32[]{:S(2)}, u32[]{:S(2)}) collective-permute-start(bf16[160,128]{1,0:T(8,128)(2,1)S(1)} %get-tuple-element.42), channel_id=1, source_target_pairs={{0,5},{1,4},{2,7},{3,6},{4,1},{5,0},{6,3},{7,2},{8,13},{9,12},{10,... | collective-permute-start | bytes 122888 | tf_op jit(solution)/shard_map/ppermute | solution.py:333
  19.3 0.0 collective-permute-start.6
  19.3 0.0 collective-permute-done.4.rest_0_
  19.3 2.0 %collective-permute-done.5.rest_1_ = bf16[160,128]{1,0:T(8,128)(2,1)S(1)} collective-permute-done((bf16[160,128]{1,0:T(8,128)(2,1)S(1)}, bf16[160,128]{1,0:T(8,128)(2,1)S(1)}, u32[]{:S(2)}, u32[]{:S(2)}) %collective-permute-start.5) | collective-permute-done | bytes 40992 | tf_op jit(solution)/shard_map/ppermute | solution.py:333
  21.3 3.8 %collective-permute-done.6.rest_2_ = bf16[160,128]{1,0:T(8,128)(2,1)S(1)} collective-permute-done((bf16[160,128]{1,0:T(8,128)(2,1)S(1)}, bf16[160,128]{1,0:T(8,128)(2,1)S(1)}, u32[]{:S(2)}, u32[]{:S(2)}) %collective-permute-start.6) | collective-permute-done | bytes 40992 | tf_op jit(solution)/shard_map/ppermute | solution.py:333
  25.1 0.1 collective-permute-start.7
  25.2 1.2 %collective-permute-done.7 = f32[8,256]{1,0:T(8,128)S(1)} collective-permute-done((f32[8,256]{1,0:T(8,128)S(1)}, f32[8,256]{1,0:T(8,128)S(1)}, u32[]{:S(2)}, u32[]{:S(2)}) %collective-permute-start.7) | collective-permute-done | bytes 8224 | tf_op jit(solution)/shard_map/ppermute | solution.py:333
  26.4 0.1 maximum_select_fusion.stats
  26.5 0.3 collective-permute-start.8
  26.8 0.1 tile.7
  26.9 0.1 broadcast_in_dim_tile.3.places
  27.0 0.7 %shard_map.123 = (bf16[12,4,128]{2,1,0:T(4,128)(2,1)S(1)}, f32[12,4,128]{2,1,0:T(4,128)S(1)}) custom-call(f32[144,128]{1,0:T(8,128)S(1)} %get-tuple-element.54.own, f32[8,256]{1,0:T(8,128)S(1)} %get-tuple-element.55.every, bf16[160,128]{1,0:T(8,128)(2,1)S(1)} %collective-permute-done.4.rest_0_, bf16[160,128]{1,0:T(8,128)(2,1)S(1)} %collective-permute-done.5.rest_1_, ...), custom_call_target="tpu_custom_call" | custom-call | tf_op jit(solution)/shard_map/pallas_call | solution.py:324
  27.7 1.1 %shard_map.121 = (bf16[1024,384]{1,0:T(8,128)(2,1)S(1)}, bf16[1024,384]{1,0:T(8,128)(2,1)S(1)}, f32[8,384]{1,0:T(8,128)S(1)}, bf16[384,128]{1,0:T(8,128)(2,1)S(1)}, bf16[384,128]{1,0:T(8,128)(2,1)S(1)}) custom-call(bf16[384,128]{1,0:T(8,128)(2,1)S(1)} %pad_maximum_fusion.gathered.mine, bf16[384,128]{1,0:T(8,128)(2,1)S(1)} %collective-permute-done.2.other, ...), custom_call_target="tpu_custom_call" | custom-call | tf_op jit(solution)/shard_map/pallas_call | solution.py:324
  28.8 1.2 %shard_map.122 = (f32[512,128]{1,0:T(8,128)S(1)}, f32[512,128]{1,0:T(8,128)S(1)}, f32[512,128]{1,0:T(8,128)S(1)}, f32[512,128]{1,0:T(8,128)S(1)}) custom-call(bf16[1024,384]{1,0:T(8,128)(2,1)S(1)} %get-tuple-element.45.probs, bf16[1024,384]{1,0:T(8,128)(2,1)S(1)} %get-tuple-element.46.slopes, f32[8,384]{1,0:T(8,128)S(1)} %get-tuple-element.47.local, ...), custom_call_target="tpu_custom_call" | custom-call | tf_op jit(solution)/shard_map/pallas_call | solution.py:324
  30.0 0.0 collective-permute-done.3.pair
  30.1 0.7 %shard_map.118 = (bf16[512,384]{1,0:T(8,128)(2,1)S(1)}, bf16[512,384]{1,0:T(8,128)(2,1)S(1)}, f32[8,384]{1,0:T(8,128)S(1)}, bf16[384,128]{1,0:T(8,128)(2,1)S(1)}, bf16[384,128]{1,0:T(8,128)(2,1)S(1)}) custom-call(bf16[768,128]{1,0:T(8,128)(2,1)S(1)} %collective-permute-done.3.pair, bf16[512,128]{1,0:T(8,128)(2,1)S(1)} %copy-done, bf16[512,128]{1,0:T(8,128)(2,1)S(1)} %copy-done.1), custom_call_target="tpu_custom_call" | custom-call | tf_op jit(solution)/shard_map/pallas_call | solution.py:324
  30.8 0.0 collective-permute-done.8.stats
  30.8 1.6 %shard_map.124 = (f32[512,128]{1,0:T(8,128)}, f32[512,128]{1,0:T(8,128)}, f32[512,128]{1,0:T(8,128)}, f32[512,128]{1,0:T(8,128)}, bf16[12,4,128]{2,1,0:T(4,128)(2,1)}, /*index=5*/f32[12,4,128]{2,1,0:T(4,128)}) custom-call(bf16[512,384]{1,0:T(8,128)(2,1)S(1)} %get-tuple-element.35.probs, bf16[512,384]{1,0:T(8,128)(2,1)S(1)} %get-tuple-element.36.slopes, ...), custom_call_target="tpu_custom_call" | custom-call | tf_op jit(solution)/shard_map/pallas_call | solution.py:324
  (9 shorter events, 0.1 us)
Async XLA Ops:
  0.6 4.3 %copy-start.4 = (bf16[1,12,4,128]{3,2,1,0:T(4,128)(2,1)S(1)}, bf16[1,12,4,128]{3,2,1,0:T(4,128)(2,1)}, u32[]{:S(2)}) copy-start(bf16[1,12,4,128]{3,2,1,0:T(4,128)(2,1)} %param.7) | copy-start | bytes 36868
  1.4 3.5 %copy-start.5 = (bf16[1,12,4,128]{3,2,1,0:T(4,128)(2,1)S(1)}, bf16[1,12,4,128]{3,2,1,0:T(4,128)(2,1)}, u32[]{:S(2)}) copy-start(bf16[1,12,4,128]{3,2,1,0:T(4,128)(2,1)} %param.8) | copy-start | bytes 36868
  1.4 5.1 %collective-permute-start = (bf16[96,128]{1,0:T(8,128)(2,1)S(1)}, bf16[96,128]{1,0:T(8,128)(2,1)S(1)}, u32[]{:S(2)}, u32[]{:S(2)}) collective-permute-start(bf16[96,128]{1,0:T(8,128)(2,1)S(1)} %pad_maximum_fusion.2), channel_id=1, source_target_pairs={{0,5},{1,4},{2,7},{3,6},{4,1},{5,0},{6,3},{7,2},{8,13},{9,12},{10,... | collective-permute-start | bytes 73736 | tf_op jit(solution)/shard_map/ppermute | solution.py:333
  6.5 3.7 %collective-permute-start.1 = (bf16[192,128]{1,0:T(8,128)(2,1)S(1)}, bf16[192,128]{1,0:T(8,128)(2,1)S(1)}, u32[]{:S(2)}, u32[]{:S(2)}) collective-permute-start(bf16[192,128]{1,0:T(8,128)(2,1)S(1)} %pad_maximum_fusion.1), channel_id=1, source_target_pairs={{0,3},{1,2},{2,1},{3,0},{4,7},{5,6},{6,5},{7,4},{8,11},{9,10},{10,... | collective-permute-start | bytes 147464 | tf_op jit(solution)/shard_map/ppermute | solution.py:333
  10.2 3.5 %copy-start.3 = (bf16[1,512,128]{2,1,0:T(8,128)(2,1)S(1)}, bf16[1,512,128]{2,1,0:T(8,128)(2,1)}, u32[]{:S(2)}) copy-start(bf16[1,512,128]{2,1,0:T(8,128)(2,1)} %param.12) | copy-start | bytes 393220
  10.2 1.4 %collective-permute-start.2 = (bf16[384,128]{1,0:T(8,128)(2,1)S(1)}, bf16[384,128]{1,0:T(8,128)(2,1)S(1)}, u32[]{:S(2)}, u32[]{:S(2)}) collective-permute-start(bf16[384,128]{1,0:T(8,128)(2,1)S(1)} %pad_maximum_fusion.gathered.mine), channel_id=1, source_target_pairs={{0,1},{1,0},{2,3},{3,2},{4,5},{5,4},{6,7},{7,6},{8,9},{9,8},{10,11... | collective-permute-start | bytes 294920 | tf_op jit(solution)/shard_map/ppermute | solution.py:333
  10.7 2.8 %copy-start.6 = (s32[1,48]{1,0:T(1,128)S(1)}, s32[1,48]{1,0:T(1,128)}, u32[]{:S(2)}) copy-start(s32[1,48]{1,0:T(1,128)} %param.13) | copy-start | bytes 580
  10.7 3.0 %copy-start.2 = (bf16[1,512,128]{2,1,0:T(8,128)(2,1)S(1)}, bf16[1,512,128]{2,1,0:T(8,128)(2,1)}, u32[]{:S(2)}) copy-start(bf16[1,512,128]{2,1,0:T(8,128)(2,1)} %param.11) | copy-start | bytes 393220
  10.7 3.0 %copy-start = (bf16[512,128]{1,0:T(8,128)(2,1)S(1)}, bf16[512,128]{1,0:T(8,128)(2,1)}, u32[]{:S(2)}) copy-start(bf16[512,128]{1,0:T(8,128)(2,1)} %root_k.5) | copy-start | bytes 393220
  10.7 3.0 %copy-start.1 = (bf16[512,128]{1,0:T(8,128)(2,1)S(1)}, bf16[512,128]{1,0:T(8,128)(2,1)}, u32[]{:S(2)}) copy-start(bf16[512,128]{1,0:T(8,128)(2,1)} %root_v.5) | copy-start | bytes 393220
  11.7 18.4 %collective-permute-start.3 = (bf16[768,128]{1,0:T(8,128)(2,1)S(1)}, bf16[768,128]{1,0:T(8,128)(2,1)S(1)}, u32[]{:S(2)}, u32[]{:S(2)}) collective-permute-start(bf16[768,128]{1,0:T(8,128)(2,1)S(1)} %constant_dynamic-update-slice_fusion), channel_id=1, source_target_pairs={{0,9},{1,8},{8,1},{9,0},{2,11},{3,10},{10,3},{11,2},{4,13},{5,12},... | collective-permute-start | bytes 589832 | tf_op jit(solution)/shard_map/ppermute | solution.py:333
  14.7 4.6 %collective-permute-start.4 = (bf16[160,128]{1,0:T(8,128)(2,1)S(1)}, bf16[160,128]{1,0:T(8,128)(2,1)S(1)}, u32[]{:S(2)}, u32[]{:S(2)}) collective-permute-start(bf16[160,128]{1,0:T(8,128)(2,1)S(1)} %get-tuple-element.41), channel_id=1, source_target_pairs={{0,3},{1,2},{2,1},{3,0},{4,7},{5,6},{6,5},{7,4},{8,11},{9,10},{10,... | collective-permute-start | bytes 122888 | tf_op jit(solution)/shard_map/ppermute | solution.py:333
  16.3 5.0 %collective-permute-start.5 = (bf16[160,128]{1,0:T(8,128)(2,1)S(1)}, bf16[160,128]{1,0:T(8,128)(2,1)S(1)}, u32[]{:S(2)}, u32[]{:S(2)}) collective-permute-start(bf16[160,128]{1,0:T(8,128)(2,1)S(1)} %get-tuple-element.42), channel_id=1, source_target_pairs={{0,5},{1,4},{2,7},{3,6},{4,1},{5,0},{6,3},{7,2},{8,13},{9,12},{10,... | collective-permute-start | bytes 122888 | tf_op jit(solution)/shard_map/ppermute | solution.py:333
  19.3 5.8 %collective-permute-start.6 = (bf16[160,128]{1,0:T(8,128)(2,1)S(1)}, bf16[160,128]{1,0:T(8,128)(2,1)S(1)}, u32[]{:S(2)}, u32[]{:S(2)}) collective-permute-start(bf16[160,128]{1,0:T(8,128)(2,1)S(1)} %get-tuple-element.43), channel_id=1, source_target_pairs={{0,6},{1,7},{2,4},{3,5},{4,2},{5,3},{6,0},{7,1},{8,14},{9,15},{10,... | collective-permute-start | bytes 122888 | tf_op jit(solution)/shard_map/ppermute | solution.py:333
  25.1 1.2 %collective-permute-start.7 = (f32[8,256]{1,0:T(8,128)S(1)}, f32[8,256]{1,0:T(8,128)S(1)}, u32[]{:S(2)}, u32[]{:S(2)}) collective-permute-start(f32[8,256]{1,0:T(8,128)S(1)} %get-tuple-element.44), channel_id=1, source_target_pairs={{0,1},{1,0},{2,3},{3,2},{4,5},{5,4},{6,7},{7,6},{8,9},{9,8},{10,11... | collective-permute-start | bytes 24584 | tf_op jit(solution)/shard_map/ppermute | solution.py:333
  26.5 4.3 %collective-permute-start.8 = (f32[8,384]{1,0:T(8,128)S(1)}, f32[8,384]{1,0:T(8,128)S(1)}, u32[]{:S(2)}, u32[]{:S(2)}) collective-permute-start(f32[8,384]{1,0:T(8,128)S(1)} %maximum_select_fusion.stats), channel_id=1, source_target_pairs={{0,9},{1,8},{8,1},{9,0},{2,11},{3,10},{10,3},{11,2},{4,13},{5,12},... | collective-permute-start | bytes 36872 | tf_op jit(solution)/shard_map/ppermute | solution.py:333

commit v2 on v1

--- a/solution.py
+++ b/solution.py
@@ -58,6 +58,29 @@
         query[pl.ds(to, lay.rows), :] = source[pl.ds(start, lay.rows), :]
         start = pl.multiple_of(base + at * (2 * lay.rows) + lay.rows, 16)
         grad[pl.ds(to, lay.rows), :] = source[pl.ds(start, lay.rows), :]
+
+
+def prepare_kernel(root_k, root_v, branch_k, branch_v, positions,
+                   to_rk, to_rv, to_bk, to_bv, column, row, hold, sems, *, lay):
+    copies = [pltpu.make_async_copy(source, target, sems.at[n]) for n, (source, target) in enumerate(
+        [(positions, hold), (root_k, to_rk), (root_v, to_rv), (branch_k, to_bk), (branch_v, to_bv)])]
+    for copy in copies:
+        copy.start()
+    copies[0].wait()
+    answers = hold.shape[1]
+    known = hold[0:1, :].astype(f32)
+    each = lay.total // answers
+    for at in range(0, column.shape[0], LANES):
+        size = min(LANES, column.shape[0] - at)
+        spot = at + lax.broadcasted_iota(jnp.int32, (size, answers), 0)
+        spot = jnp.where(spot >= lay.total, spot - lay.total, spot)
+        first = each * lax.broadcasted_iota(jnp.int32, (size, answers), 1)
+        mine = jnp.where((spot >= first) & (spot < first + each), known, 0.0)
+        found = jnp.sum(mine, axis=1, keepdims=True)
+        column[at:at + size, :] = found.astype(jnp.int32)
+        row[:, at:at + size] = jnp.broadcast_to(found, (size, LANES)).T[0:8, 0:size].astype(jnp.int32)
+    for copy in copies[1:]:
+        copy.wait()
 
 
 def split3(value):
@@ -310,27 +333,26 @@
         self.count, self.rows, self.scale = count, rows, scale
         self.total = count * rows
         self.tiles = lane_tiles(self.total)
-        self.bits = list(reversed(range(count.bit_length() - 1)))
+        self.bits = list(range(count.bit_length() - 1))
         self.swap = count <= 4
 
 
 VMEM = pl.BlockSpec(memory_space=pltpu.VMEM)
 ANY = pl.BlockSpec(memory_space=pl.ANY)
-
-
-def call(kernel, lay, args, outs, scratch=(), away=0):
+HBM = pl.BlockSpec(memory_space=pltpu.HBM)
+
+
+def call(kernel, lay, args, outs, scratch=(), away=0, far=False):
     specs = [VMEM] * (len(outs) - away) + [ANY] * away
     limit = (20 if lay.total <= 384 else 50) * 2**20
+    if far:
+        args = [pltpu.with_memory_space_constraint(value, pltpu.HBM) for value in args]
     return pl.pallas_call(
         functools.partial(kernel, lay=lay),
         out_shape=[jax.ShapeDtypeStruct(shape, kind) for shape, kind in outs],
-        in_specs=[VMEM] * len(args), out_specs=specs, scratch_shapes=list(scratch),
+        in_specs=[HBM if far else VMEM] * len(args), out_specs=specs, scratch_shapes=list(scratch),
         compiler_params=pltpu.CompilerParams(vmem_limit_bytes=limit),
     )(*args)
-
-
-def move(value, axis, pairs):
-    return lax.ppermute(value, axis, pairs)
 
 
 def per_device(mesh, queries, output_cotangent, root_keys, root_values,
@@ -349,12 +371,8 @@
     lanes = heads * total
     root_count = root_keys.shape[0]
     branch_count = branch_keys.shape[1]
-    branch_k, branch_v = branch_keys[0], branch_values[0]
     seq_index = lax.axis_index("seq")
     head_index = lax.axis_index("head")
-    places = jnp.repeat(answer_positions[0], heads_here)
-    place_column = places[:, None]
-    place_row = jnp.tile(places, heads)[None, :]
     crossing = lay.swap and heads == 2
 
     def seq_pairs(m):
@@ -369,10 +387,20 @@
     shifts = range(1, branches)
 
     gathered = jnp.concatenate([queries.reshape(rows, width), output_cotangent.reshape(rows, width)], 0)
-    for bit in lay.bits:
-        pairs = seq_pairs(1 << bit)
-        gathered = jnp.concatenate([gathered, move(gathered, ("seq", "head"), pairs)], 0)
-    other = move(gathered, "head", swap_heads)
+    gathered = lax.optimization_barrier(gathered)
+    if lay.swap:
+        gathered = jnp.concatenate([gathered] + [
+            lax.ppermute(gathered, ("seq", "head"), seq_pairs(m)) for m in range(1, count)], 0)
+    else:
+        for bit in lay.bits:
+            pairs = seq_pairs(1 << bit)
+            gathered = jnp.concatenate([gathered, lax.ppermute(gathered, ("seq", "head"), pairs)], 0)
+    keys = [((root_count, width), bf16)] * 2 + [((branch_count, width), bf16)] * 2
+    root_k, root_v, branch_k, branch_v, place_column, place_row = call(
+        prepare_kernel, lay, (root_keys, root_values, branch_keys[0], branch_values[0], answer_positions),
+        keys + [((lanes, 1), jnp.int32), ((8, lanes), jnp.int32)],
+        [pltpu.VMEM(answer_positions.shape, jnp.int32), pltpu.SemaphoreType.DMA((5,))], far=True)
+    other = lax.ppermute(gathered, "head", swap_heads)
 
     message_rows = 3 * rows + 8 * tiles
     if lay.swap:
@@ -381,12 +409,12 @@
         message_shapes = [((count, message_rows, width), bf16)]
     own, coded, *messages = call(
         forward_kernel, lay,
-        (gathered, root_keys, root_values, branch_k, branch_v, place_column),
+        (gathered, root_k, root_v, branch_k, branch_v, place_column),
         [((3 * rows, width), f32), ((8, tiles * LANES), f32)] + message_shapes,
         [pltpu.VMEM((3, total, width), f32), pltpu.VMEM((total, width), bf16),
          pltpu.VMEM((total, width), bf16)])
     if lay.swap:
-        received = [move(message, ("seq", "head"), seq_pairs(m + 1))
+        received = [lax.ppermute(message, ("seq", "head"), seq_pairs(m + 1))
                     for m, message in enumerate(messages)]
     else:
         whole = lax.all_to_all(messages[0], "seq", split_axis=0, concat_axis=0, tiled=True)
@@ -394,7 +422,7 @@
                     for m in range(1, count)]
 
     pair = jnp.concatenate([gathered, other], 0)
-    far = [move(pair, ("branch", "head"), far_pairs(m, FAR_FLIP if heads == 2 else 0)) for m in shifts]
+    far = [lax.ppermute(pair, ("branch", "head"), far_pairs(m, FAR_FLIP if heads == 2 else 0)) for m in shifts]
 
     def weights_shapes(keys):
         shapes = [((keys, lanes), bf16), ((keys, lanes), bf16), ((8, lanes), f32),
@@ -404,16 +432,16 @@
 
     shapes, scratch = weights_shapes(branch_count + root_count)
     own_pre = call(own_pre_kernel, lay,
-                   (gathered, other, place_row, root_keys, root_values, branch_k, branch_v),
+                   (gathered, other, place_row, root_k, root_v, branch_k, branch_v),
                    shapes, scratch)
 
     tall = -(-2 * count // 8) * 8
     final, every = call(combine_kernel, lay, (coded, *received),
                         [((8, tiles * LANES), f32), ((tall, tiles * LANES), f32)])
-    other_final = move(final, "head", swap_heads)
+    other_final = lax.ppermute(final, "head", swap_heads)
     a, b = final[:, :total], other_final[:, :total]
     stats = jnp.where(head_index == 0, jnp.concatenate([a, b], 1), jnp.concatenate([b, a], 1))
-    far_stats = [move(stats, ("branch", "head"), far_pairs(m, STAT_FLIP if heads == 2 else 0)) for m in shifts]
+    far_stats = [lax.ppermute(stats, ("branch", "head"), far_pairs(m, STAT_FLIP if heads == 2 else 0)) for m in shifts]
 
     def final_scratch(keys):
         blocks = -(-keys // 256)
@@ -432,7 +460,7 @@
         [root_sum, root_sum, branch_sum, branch_sum], first)
     shapes, scratch = weights_shapes(root_count)
     for pair, pair_stats in zip(far, far_stats):
-        pre = call(other_pre_kernel, lay, (pair, root_keys, root_values),
+        pre = call(other_pre_kernel, lay, (pair, root_k, root_v),
                    shapes, scratch)
         acc_k, acc_v, branch_gk, branch_gv, attention, query_grad = call(
             other_final_kernel, lay,

time: 32.7 us -> 31.9 us (0.976)
  starting transfers between devices: 12.7 us -> 11.3 us
  Pallas kernels: 6.41 us -> 7.56 us
  local copies, waits for them, and re-layouts: 0.41 us -> 0.05 us
    ppermute x9 -> x10, starting transfers between devices: 12.7 us -> 11.3 us  [the longest x3 5.36 us: body(): lax.ppermute(gathered, ('seq', 'head'), seq_pairs(m))]
    pallas_call x7 -> x8, Pallas kernels: 6.41 us -> 7.56 us  [call(): pl.pallas_call(functools.partial(kernel, lay=lay), out_shape=[jax.ShapeDt...]
    ppermute x9 -> x10, waiting for transfers between devices: 11.3 us -> 11.1 us  [the longest x3 5.61 us: body(): lax.ppermute(gathered, ('seq', 'head'), seq_pairs(m))]
  transfers between devices with their start and end apart: 9 -> 10, of which waited for: 6 -> 6; matrix products, arithmetic and copies ran while one was open for 1% -> 0% of each run, Pallas kernels for 15% -> 19%
where the time goes in v2:
time: 31.9 us; the launch traced here: 31.5 us
  starting transfers between devices  11.3 us (35%)
  waiting for transfers between devices  11.1 us (35%)
  Pallas kernels  7.56 us (24%)
  other arithmetic  0.81 us (3%)
  between operations  0.76 us (2%)
    pallas_call x8, Pallas kernels, call(): pl.pallas_call(functools.partial(kernel, lay=lay), out_shape=[jax.ShapeDt...  7.56 us
    ppermute x3, waiting for transfers between devices, body(): lax.ppermute(gathered, ('seq', 'head'), seq_pairs(m))  5.61 us
    ppermute x3, starting transfers between devices, body(): lax.ppermute(gathered, ('seq', 'head'), seq_pairs(m))  5.36 us
    ppermute x3, starting transfers between devices, body(): lax.ppermute(message, ('seq', 'head'), seq_pairs(m + 1))  4.16 us
    ppermute x3, waiting for transfers between devices, body(): lax.ppermute(message, ('seq', 'head'), seq_pairs(m + 1))  3.06 us
    ppermute x1, starting transfers between devices, body(): lax.ppermute(pair, ('branch', 'head'), far_pairs(m, FAR_FLIP if heads ==...  1.31 us
    ppermute x1, waiting for transfers between devices, body(): other = lax.ppermute(gathered, 'head', swap_heads)  1.25 us
    ppermute x1, waiting for transfers between devices, body(): other_final = lax.ppermute(final, 'head', swap_heads)  1.15 us
  transfers between devices with their start and end apart: 10, of which 6 were waited for; matrix products, arithmetic and copies ran while one was open for 0% of the time, Pallas kernels for 19%

profile of v2, /device:TPU:0, one launch (start us, length us, event | category | flops | bytes accessed | tf_op | source)
XLA Modules:
  0.0 31.5 jit_solution(2317426169831478753)
XLA Ops:
  0.6 0.7 %pad_maximum_fusion.1 = bf16[96,128]{1,0:T(8,128)(2,1)S(1)} fusion(bf16[48,128]{1,0:T(8,128)(2,1)} %bitcast.13, bf16[48,128]{1,0:T(8,128)(2,1)} %bitcast.14), kind=kLoop, calls=%fused_computation.1 | loop fusion | flops 49152 | bytes 49152 | tf_op jit(solution)/shard_map/concatenate | solution.py:389
  1.4 2.5 %collective-permute-start = (bf16[96,128]{1,0:T(8,128)(2,1)S(1)}, bf16[96,128]{1,0:T(8,128)(2,1)S(1)}, u32[]{:S(2)}, u32[]{:S(2)}) collective-permute-start(bf16[96,128]{1,0:T(8,128)(2,1)S(1)} %pad_maximum_fusion.1), channel_id=1, source_target_pairs={{0,3},{1,2},{2,1},{3,0},{4,7},{5,6},{6,5},{7,4},{8,11},{9,10},{10,... | collective-permute-start | bytes 73736 | tf_op jit(solution)/shard_map/ppermute | solution.py:393
  3.9 2.9 %collective-permute-start.1 = (bf16[96,128]{1,0:T(8,128)(2,1)S(1)}, bf16[96,128]{1,0:T(8,128)(2,1)S(1)}, u32[]{:S(2)}, u32[]{:S(2)}) collective-permute-start(bf16[96,128]{1,0:T(8,128)(2,1)S(1)} %pad_maximum_fusion.1), channel_id=1, source_target_pairs={{0,5},{1,4},{2,7},{3,6},{4,1},{5,0},{6,3},{7,2},{8,13},{9,12},{10,... | collective-permute-start | bytes 73736 | tf_op jit(solution)/shard_map/ppermute | solution.py:393
  6.7 0.0 collective-permute-start.2
  6.7 0.0 collective-permute-done
  6.7 1.5 %collective-permute-done.1 = bf16[96,128]{1,0:T(8,128)(2,1)S(1)} collective-permute-done((bf16[96,128]{1,0:T(8,128)(2,1)S(1)}, bf16[96,128]{1,0:T(8,128)(2,1)S(1)}, u32[]{:S(2)}, u32[]{:S(2)}) %collective-permute-start.1) | collective-permute-done | bytes 24608 | tf_op jit(solution)/shard_map/ppermute | solution.py:393
  8.2 4.1 %collective-permute-done.2 = bf16[96,128]{1,0:T(8,128)(2,1)S(1)} collective-permute-done((bf16[96,128]{1,0:T(8,128)(2,1)S(1)}, bf16[96,128]{1,0:T(8,128)(2,1)S(1)}, u32[]{:S(2)}, u32[]{:S(2)}) %collective-permute-start.2) | collective-permute-done | bytes 24608 | tf_op jit(solution)/shard_map/ppermute | solution.py:393
  12.4 0.1 collective-permute-start.3
  12.5 1.2 %collective-permute-done.3.other = bf16[384,128]{1,0:T(8,128)(2,1)S(1)} collective-permute-done((bf16[384,128]{1,0:T(8,128)(2,1)S(1)}, bf16[384,128]{1,0:T(8,128)(2,1)S(1)}, u32[]{:S(2)}, u32[]{:S(2)}) %collective-permute-start.3) | collective-permute-done | bytes 98336 | tf_op jit(solution)/shard_map/ppermute | solution.py:403
  13.7 1.3 %collective-permute-start.4 = (bf16[768,128]{1,0:T(8,128)(2,1)S(1)}, bf16[768,128]{1,0:T(8,128)(2,1)S(1)}, u32[]{:S(2)}, u32[]{:S(2)}) collective-permute-start(bf16[768,128]{1,0:T(8,128)(2,1)S(1)} %constant_dynamic-update-slice_fusion), channel_id=1, source_target_pairs={{0,9},{1,8},{8,1},{9,0},{2,11},{3,10},{10,3},{11,2},{4,13},{5,12},... | collective-permute-start | bytes 589832 | tf_op jit(solution)/shard_map/ppermute | solution.py:425
  15.1 1.2 %shard_map.118 = (bf16[512,128]{1,0:T(8,128)(2,1)S(1)}, bf16[512,128]{1,0:T(8,128)(2,1)S(1)}, bf16[512,128]{1,0:T(8,128)(2,1)S(1)}, bf16[512,128]{1,0:T(8,128)(2...) custom-call(bf16[512,128]{1,0:T(8,128)(2,1)} %root_k.1, bf16[512,128]{1,0:T(8,128)(2,1)} %root_v.1, ...), custom_call_target="tpu_custom_call" | custom-call | tf_op jit(solution)/shard_map/pallas_call | solution.py:350
  16.2 1.0 %shard_map.120 = (f32[144,128]{1,0:T(8,128)S(1)}, f32[8,256]{1,0:T(8,128)S(1)}, bf16[160,128]{1,0:T(8,128)(2,1)S(1)}, bf16[160,128]{1,0:T(8,128)(2,1)S(1)}, bf16[160,128]{1,0:T(8,128)(2,1)S(1)}) custom-call(bf16[384,128]{1,0:T(8,128)(2,1)S(1)} %pad_maximum_fusion.gathered.mine, bf16[512,128]{1,0:T(8,128)(2,1)S(1)} %get-tuple-element.41.root_k, ...), custom_call_target="tpu_custom_call" | custom-call | tf_op jit(solution)/shard_map/pallas_call | solution.py:350
  17.2 0.1 collective-permute-start.5
  17.3 0.5 %collective-permute-start.6 = (bf16[160,128]{1,0:T(8,128)(2,1)S(1)}, bf16[160,128]{1,0:T(8,128)(2,1)S(1)}, u32[]{:S(2)}, u32[]{:S(2)}) collective-permute-start(bf16[160,128]{1,0:T(8,128)(2,1)S(1)} %get-tuple-element.53), channel_id=1, source_target_pairs={{0,5},{1,4},{2,7},{3,6},{4,1},{5,0},{6,3},{7,2},{8,13},{9,12},{10,... | collective-permute-start | bytes 122888 | tf_op jit(solution)/shard_map/ppermute | solution.py:417
  17.8 3.5 %collective-permute-start.7 = (bf16[160,128]{1,0:T(8,128)(2,1)S(1)}, bf16[160,128]{1,0:T(8,128)(2,1)S(1)}, u32[]{:S(2)}, u32[]{:S(2)}) collective-permute-start(bf16[160,128]{1,0:T(8,128)(2,1)S(1)} %get-tuple-element.54), channel_id=1, source_target_pairs={{0,6},{1,7},{2,4},{3,5},{4,2},{5,3},{6,0},{7,1},{8,14},{9,15},{10,... | collective-permute-start | bytes 122888 | tf_op jit(solution)/shard_map/ppermute | solution.py:417
  21.4 0.0 collective-permute-done.5.rest_0_
  21.4 0.3 collective-permute-done.6.rest_1_
  21.6 2.8 %collective-permute-done.7.rest_2_ = bf16[160,128]{1,0:T(8,128)(2,1)S(1)} collective-permute-done((bf16[160,128]{1,0:T(8,128)(2,1)S(1)}, bf16[160,128]{1,0:T(8,128)(2,1)S(1)}, u32[]{:S(2)}, u32[]{:S(2)}) %collective-permute-start.7) | collective-permute-done | bytes 40992 | tf_op jit(solution)/shard_map/ppermute | solution.py:417
  24.4 0.1 collective-permute-start.8
  24.5 1.2 %collective-permute-done.8 = f32[8,256]{1,0:T(8,128)S(1)} collective-permute-done((f32[8,256]{1,0:T(8,128)S(1)}, f32[8,256]{1,0:T(8,128)S(1)}, u32[]{:S(2)}, u32[]{:S(2)}) %collective-permute-start.8) | collective-permute-done | bytes 8224 | tf_op jit(solution)/shard_map/ppermute | solution.py:441
  25.7 0.1 maximum_select_fusion.stats
  25.8 0.3 collective-permute-start.9
  26.1 0.7 %shard_map.124 = (bf16[12,4,128]{2,1,0:T(4,128)(2,1)S(1)}, f32[12,4,128]{2,1,0:T(4,128)S(1)}) custom-call(f32[144,128]{1,0:T(8,128)S(1)} %get-tuple-element.66.own, f32[8,256]{1,0:T(8,128)S(1)} %get-tuple-element.67.every, bf16[160,128]{1,0:T(8,128)(2,1)S(1)} %collective-permute-done.5.rest_0_, bf16[160,128]{1,0:T(8,128)(2,1)S(1)} %collective-permute-done.6.rest_1_, ...), custom_call_target="tpu_custom_call" | custom-call | tf_op jit(solution)/shard_map/pallas_call | solution.py:350
  26.8 1.1 %shard_map.122 = (bf16[1024,384]{1,0:T(8,128)(2,1)S(1)}, bf16[1024,384]{1,0:T(8,128)(2,1)S(1)}, f32[8,384]{1,0:T(8,128)S(1)}, bf16[384,128]{1,0:T(8,128)(2,1)S(1)}, bf16[384,128]{1,0:T(8,128)(2,1)S(1)}) custom-call(bf16[384,128]{1,0:T(8,128)(2,1)S(1)} %pad_maximum_fusion.gathered.mine, bf16[384,128]{1,0:T(8,128)(2,1)S(1)} %collective-permute-done.3.other, ...), custom_call_target="tpu_custom_call" | custom-call | tf_op jit(solution)/shard_map/pallas_call | solution.py:350
  27.9 1.2 %shard_map.123 = (f32[512,128]{1,0:T(8,128)S(1)}, f32[512,128]{1,0:T(8,128)S(1)}, f32[512,128]{1,0:T(8,128)S(1)}, f32[512,128]{1,0:T(8,128)S(1)}) custom-call(bf16[1024,384]{1,0:T(8,128)(2,1)S(1)} %get-tuple-element.57.probs, bf16[1024,384]{1,0:T(8,128)(2,1)S(1)} %get-tuple-element.58.slopes, f32[8,384]{1,0:T(8,128)S(1)} %get-tuple-element.59.local, ...), custom_call_target="tpu_custom_call" | custom-call | tf_op jit(solution)/shard_map/pallas_call | solution.py:350
  29.2 0.0 collective-permute-done.4.pair
  29.2 0.7 %shard_map.119 = (bf16[512,384]{1,0:T(8,128)(2,1)S(1)}, bf16[512,384]{1,0:T(8,128)(2,1)S(1)}, f32[8,384]{1,0:T(8,128)S(1)}, bf16[384,128]{1,0:T(8,128)(2,1)S(1)}, bf16[384,128]{1,0:T(8,128)(2,1)S(1)}) custom-call(bf16[768,128]{1,0:T(8,128)(2,1)S(1)} %collective-permute-done.4.pair, bf16[512,128]{1,0:T(8,128)(2,1)S(1)} %get-tuple-element.41.root_k, ...), custom_call_target="tpu_custom_call" | custom-call | tf_op jit(solution)/shard_map/pallas_call | solution.py:350
  29.9 0.0 collective-permute-done.9.stats
  29.9 1.6 %shard_map.125 = (f32[512,128]{1,0:T(8,128)}, f32[512,128]{1,0:T(8,128)}, f32[512,128]{1,0:T(8,128)}, f32[512,128]{1,0:T(8,128)}, bf16[12,4,128]{2,1,0:T(4,128)(2,1)}, /*index=5*/f32[12,4,128]{2,1,0:T(4,128)}) custom-call(bf16[512,384]{1,0:T(8,128)(2,1)S(1)} %get-tuple-element.43.probs, bf16[512,384]{1,0:T(8,128)(2,1)S(1)} %get-tuple-element.44.slopes, ...), custom_call_target="tpu_custom_call" | custom-call | tf_op jit(solution)/shard_map/pallas_call | solution.py:350
  (7 shorter events, 0.1 us)
Async XLA Ops:
  1.4 5.4 %collective-permute-start = (bf16[96,128]{1,0:T(8,128)(2,1)S(1)}, bf16[96,128]{1,0:T(8,128)(2,1)S(1)}, u32[]{:S(2)}, u32[]{:S(2)}) collective-permute-start(bf16[96,128]{1,0:T(8,128)(2,1)S(1)} %pad_maximum_fusion.1), channel_id=1, source_target_pairs={{0,3},{1,2},{2,1},{3,0},{4,7},{5,6},{6,5},{7,4},{8,11},{9,10},{10,... | collective-permute-start | bytes 73736 | tf_op jit(solution)/shard_map/ppermute | solution.py:393
  3.9 4.4 %collective-permute-start.1 = (bf16[96,128]{1,0:T(8,128)(2,1)S(1)}, bf16[96,128]{1,0:T(8,128)(2,1)S(1)}, u32[]{:S(2)}, u32[]{:S(2)}) collective-permute-start(bf16[96,128]{1,0:T(8,128)(2,1)S(1)} %pad_maximum_fusion.1), channel_id=1, source_target_pairs={{0,5},{1,4},{2,7},{3,6},{4,1},{5,0},{6,3},{7,2},{8,13},{9,12},{10,... | collective-permute-start | bytes 73736 | tf_op jit(solution)/shard_map/ppermute | solution.py:393
  6.7 5.6 %collective-permute-start.2 = (bf16[96,128]{1,0:T(8,128)(2,1)S(1)}, bf16[96,128]{1,0:T(8,128)(2,1)S(1)}, u32[]{:S(2)}, u32[]{:S(2)}) collective-permute-start(bf16[96,128]{1,0:T(8,128)(2,1)S(1)} %pad_maximum_fusion.1), channel_id=1, source_target_pairs={{0,6},{1,7},{2,4},{3,5},{4,2},{5,3},{6,0},{7,1},{8,14},{9,15},{10,... | collective-permute-start | bytes 73736 | tf_op jit(solution)/shard_map/ppermute | solution.py:393
  12.4 1.4 %collective-permute-start.3 = (bf16[384,128]{1,0:T(8,128)(2,1)S(1)}, bf16[384,128]{1,0:T(8,128)(2,1)S(1)}, u32[]{:S(2)}, u32[]{:S(2)}) collective-permute-start(bf16[384,128]{1,0:T(8,128)(2,1)S(1)} %pad_maximum_fusion.gathered.mine), channel_id=1, source_target_pairs={{0,1},{1,0},{2,3},{3,2},{4,5},{5,4},{6,7},{7,6},{8,9},{9,8},{10,11... | collective-permute-start | bytes 294920 | tf_op jit(solution)/shard_map/ppermute | solution.py:403
  13.7 15.4 %collective-permute-start.4 = (bf16[768,128]{1,0:T(8,128)(2,1)S(1)}, bf16[768,128]{1,0:T(8,128)(2,1)S(1)}, u32[]{:S(2)}, u32[]{:S(2)}) collective-permute-start(bf16[768,128]{1,0:T(8,128)(2,1)S(1)} %constant_dynamic-update-slice_fusion), channel_id=1, source_target_pairs={{0,9},{1,8},{8,1},{9,0},{2,11},{3,10},{10,3},{11,2},{4,13},{5,12},... | collective-permute-start | bytes 589832 | tf_op jit(solution)/shard_map/ppermute | solution.py:425
  17.2 4.2 %collective-permute-start.5 = (bf16[160,128]{1,0:T(8,128)(2,1)S(1)}, bf16[160,128]{1,0:T(8,128)(2,1)S(1)}, u32[]{:S(2)}, u32[]{:S(2)}) collective-permute-start(bf16[160,128]{1,0:T(8,128)(2,1)S(1)} %get-tuple-element.52), channel_id=1, source_target_pairs={{0,3},{1,2},{2,1},{3,0},{4,7},{5,6},{6,5},{7,4},{8,11},{9,10},{10,... | collective-permute-start | bytes 122888 | tf_op jit(solution)/shard_map/ppermute | solution.py:417
  17.3 4.4 %collective-permute-start.6 = (bf16[160,128]{1,0:T(8,128)(2,1)S(1)}, bf16[160,128]{1,0:T(8,128)(2,1)S(1)}, u32[]{:S(2)}, u32[]{:S(2)}) collective-permute-start(bf16[160,128]{1,0:T(8,128)(2,1)S(1)} %get-tuple-element.53), channel_id=1, source_target_pairs={{0,5},{1,4},{2,7},{3,6},{4,1},{5,0},{6,3},{7,2},{8,13},{9,12},{10,... | collective-permute-start | bytes 122888 | tf_op jit(solution)/shard_map/ppermute | solution.py:417
  17.8 6.6 %collective-permute-start.7 = (bf16[160,128]{1,0:T(8,128)(2,1)S(1)}, bf16[160,128]{1,0:T(8,128)(2,1)S(1)}, u32[]{:S(2)}, u32[]{:S(2)}) collective-permute-start(bf16[160,128]{1,0:T(8,128)(2,1)S(1)} %get-tuple-element.54), channel_id=1, source_target_pairs={{0,6},{1,7},{2,4},{3,5},{4,2},{5,3},{6,0},{7,1},{8,14},{9,15},{10,... | collective-permute-start | bytes 122888 | tf_op jit(solution)/shard_map/ppermute | solution.py:417
  24.4 1.2 %collective-permute-start.8 = (f32[8,256]{1,0:T(8,128)S(1)}, f32[8,256]{1,0:T(8,128)S(1)}, u32[]{:S(2)}, u32[]{:S(2)}) collective-permute-start(f32[8,256]{1,0:T(8,128)S(1)} %get-tuple-element.55), channel_id=1, source_target_pairs={{0,1},{1,0},{2,3},{3,2},{4,5},{5,4},{6,7},{7,6},{8,9},{9,8},{10,11... | collective-permute-start | bytes 24584 | tf_op jit(solution)/shard_map/ppermute | solution.py:441
  25.8 4.1 %collective-permute-start.9 = (f32[8,384]{1,0:T(8,128)S(1)}, f32[8,384]{1,0:T(8,128)S(1)}, u32[]{:S(2)}, u32[]{:S(2)}) collective-permute-start(f32[8,384]{1,0:T(8,128)S(1)} %maximum_select_fusion.stats), channel_id=1, source_target_pairs={{0,9},{1,8},{8,1},{9,0},{2,11},{3,10},{10,3},{11,2},{4,13},{5,12},... | collective-permute-start | bytes 36872 | tf_op jit(solution)/shard_map/ppermute | solution.py:444
